TPU v7x, 32 devices: a whole 2x2x4 slice. The times are simulated.
32 devices in a mesh: gx: 4 (over y, core), gz: 2 (over x), ta: 4 (over z).
Axes of the slice: x: 2, y: 2, z: 4, core: 2. Of those that a mesh axis runs over, the one named last changes fastest.
Arguments:
- links: float32 [4, 2, 3, 3, 16, 8, 512], P(None, None, None, None, 'ta', 'gz', 'gx'), may hold values from -1 to 1, as said below
Outputs:
- force: float32 [4, 2, 3, 3, 16, 8, 512], P(None, None, None, None, 'ta', 'gz', 'gx')
Inputs may be any that keep to these rules, and one draw needn't show every extreme that they name: Every link matrix (real part links[mu, 0], imaginary part links[mu, 1]) is special unitary, up to float32 rounding.
All inputs are finite; a program needn't handle non-finite values.
Results may differ from a plain program's by a relative error of at most 0.0003.
Values sent between devices are 32-bit elements; how exact they have to be, the bound alone decides.
A program may use at most 64 MiB of HBM per device.

v0:
```python
import functools

import jax
import jax.numpy as jnp
from jax import lax
from jax.experimental import pallas as pl
from jax.experimental.pallas import tpu as pltpu
from jax.sharding import PartitionSpec as P

NX = 16
COEFF = -1.9
AXES = ("ta", "gz", "gx")
SUB, LANES = 8, 128


def others(d):
    return [m for m in range(4) if m != d]


class Lattice:
    def __init__(self, depth):
        self.depth = depth
        self.per = SUB // depth
        self.ygroups = LANES // NX
        self.row = lax.broadcasted_iota(jnp.int32, (SUB, LANES), 0)
        self.lane = lax.broadcasted_iota(jnp.int32, (SUB, LANES), 1)
        self.zrow = self.row % depth
        self.xcol = self.lane % NX

    def rows(self, value, shift):
        shift %= SUB
        return pltpu.roll(value, shift, 0) if shift else value

    def lanes(self, value, shift):
        shift %= LANES
        return pltpu.roll(value, shift, 1) if shift else value


def entry(left, right, i, j, part, left_h, right_h):
    total = None
    for k in range(3):
        li = (k, i) if left_h else (i, k)
        ri = (j, k) if right_h else (k, j)
        lr, lm = left[0][li[0]][li[1]], left[1][li[0]][li[1]]
        rr, rm = right[0][ri[0]][ri[1]], right[1][ri[0]][ri[1]]
        if part == 0:
            first, second = lr * rr, lm * rm
            minus = left_h == right_h
        elif left_h:
            first, second = lr * rm, lm * rr
            minus = True
        else:
            first, second = lm * rr, lr * rm
            minus = right_h
        value = first - second if minus else first + second
        total = value if total is None else total + value
    return total


def product(left, right, left_h=False, right_h=False):
    return [
        [[entry(left, right, i, j, part, left_h, right_h) for j in range(3)] for i in range(3)]
        for part in range(2)
    ]


def projected(left, right, left_h=False, right_h=False):
    get = lambda i, j, part: entry(left, right, i, j, part, left_h, right_h)
    pairs = ((0, 1), (0, 2), (1, 2))
    real = [get(i, j, 0) - get(j, i, 0) for i, j in pairs]
    imag = [get(i, j, 1) + get(j, i, 1) for i, j in pairs]
    diag = [get(i, i, 1) for i in range(3)]
    third = (diag[0] + diag[1] + diag[2]) * (1.0 / 3.0)
    return real + imag + [diag[0] - third, diag[1] - third]


def third_row(real, imag):
    rows_r, rows_i = [], []
    for column in range(3):
        n, l = (column + 1) % 3, (column + 2) % 3
        rows_r.append(
            real[0][n] * real[1][l]
            - imag[0][n] * imag[1][l]
            - real[0][l] * real[1][n]
            + imag[0][l] * imag[1][n]
        )
        rows_i.append(
            real[0][l] * imag[1][n]
            + imag[0][l] * real[1][n]
            - real[0][n] * imag[1][l]
            - imag[0][n] * real[1][l]
        )
    return rows_r, rows_i


def sizes(depth, halves):
    yg = LANES // NX
    per = SUB // depth

    def rows(count):
        return (
            -(-count // per) * SUB,
            -(-count // depth) * SUB * halves,
            -(-count // yg) * SUB * halves,
        )

    return rows(36), rows(24)


PLANES = ((2, 3), (1, 3), (1, 2), (0, 1), (0, 2), (0, 3))


def force_terms(
    counts, depth, halves, hbm, acc,
    u, ahead_s, local_s, plaq_s, st, sz, sy, rt, rz, ry, qz, qy, pz, py, bs, br, ezs, ezr, eys, eyr,
    load_sem, send, recv,
):
    g = Lattice(depth)
    me = [lax.axis_index(a) for a in AXES]
    nxt = [lax.rem(me[i] + 1, counts[i]) for i in range(3)]
    prv = [lax.rem(me[i] + counts[i] - 1, counts[i]) for i in range(3)]

    def device(i, index):
        where = list(me)
        where[i] = index
        by = dict(zip(AXES, where))
        return (by["gx"], by["gz"], by["ta"])

    def diagonal(time, i, index):
        where = list(me)
        where[0], where[i] = time, index
        by = dict(zip(AXES, where))
        return (by["gx"], by["gz"], by["ta"])

    barrier = pltpu.get_barrier_semaphore()
    for i in (1, 2):
        for where in (diagonal(nxt[0], i, prv[i]), diagonal(prv[0], i, nxt[i])):
            pl.semaphore_signal(
                barrier, inc=1, device_id=where, device_id_type=pl.DeviceIdType.MESH
            )
    for i in range(3):
        for index in (nxt[i], prv[i]):
            pl.semaphore_signal(
                barrier, inc=1, device_id=device(i, index), device_id_type=pl.DeviceIdType.MESH
            )

    loads = {
        m: pltpu.make_async_copy(hbm.at[m, :, 0:2], u.at[m, :, 0:2], load_sem.at[m])
        for m in range(4)
    }
    last_rows = pltpu.make_async_copy(hbm.at[:, :, 2], u.at[:, :, 2], load_sem.at[4])
    for m in (3, 2, 1, 0):
        loads[m].start()
    last_rows.start()

    def load(m, part, i, j, h):
        return u[m, part, i, j, h * SUB : (h + 1) * SUB, :]

    def comps(d, m):
        return [(m, part, i, j) for part in range(2) for i in range(2) for j in range(3)]

    def all_comps(d):
        return [c for m in others(d) for c in comps(d, m)]

    def pack_t(m):
        cs, base = comps(0, m), 12 * others(0).index(m)
        for c0 in range(0, 12, g.per):
            value = None
            for k in range(g.per):
                x = g.rows(load(*cs[c0 + k], 0), depth * k)
                value = x if value is None else jnp.where(g.row >= depth * k, x, value)
            r = (base + c0) // g.per * SUB
            st[r : r + SUB, :] = value

    def pack_z(m):
        cs, base = comps(1, m), 12 * others(1).index(m)
        for c0 in range(0, 12, depth):
            for h in range(halves):
                value = None
                for k in range(depth):
                    x = g.rows(load(*cs[c0 + k], h), k)
                    value = x if value is None else jnp.where(g.zrow >= k, x, value)
                r = ((base + c0) // depth * halves + h) * SUB
                sz[r : r + SUB, :] = value

    def pack_y():
        cs = all_comps(2)
        for c0 in range(0, len(cs), g.ygroups):
            for h in range(halves):
                value = None
                for k in range(min(g.ygroups, len(cs) - c0)):
                    x = g.lanes(load(*cs[c0 + k], h), NX * k)
                    value = x if value is None else jnp.where(g.lane >= NX * k, x, value)
                r = (c0 // g.ygroups * halves + h) * SUB
                sy[r : r + SUB, :] = value

    def pack_back(m):
        cs = comps(0, m)
        for c0 in range(0, 12, g.per):
            value = None
            for k in range(g.per):
                x = g.rows(load(*cs[c0 + k], halves - 1), depth * (k + 1))
                value = x if value is None else jnp.where(g.row >= depth * k, x, value)
            r = (12 * m + c0) // g.per * SUB
            bs[r : r + SUB, :] = value

    def pack_edges():
        cs = comps(0, 0)
        for c0 in range(0, 12, SUB):
            rows = lanes = None
            for k in range(min(SUB, 12 - c0)):
                v = load(*cs[c0 + k], halves - 1)
                x = g.rows(v, k - (SUB - depth))
                rows = x if rows is None else jnp.where(g.row >= k, x, rows)
            ezs[c0 : c0 + SUB, :] = rows
        for c0 in range(0, 12, g.ygroups):
            for k in range(min(g.ygroups, 12 - c0)):
                x = g.lanes(g.rows(load(*cs[c0 + k], halves - 1), depth), NX * k)
                lanes = x if k == 0 else jnp.where(g.lane >= NX * k, x, lanes)
            r = c0 // g.ygroups * SUB
            eys[r : r + SUB, :] = lanes

    for m in (3, 2, 1, 0):
        loads[m].wait()
        pack_back(m)
        if m != 0:
            pack_t(m)
        if m != 1:
            pack_z(m)
    pack_y()
    pack_edges()

    def remote(src, dst, slot, i, index):
        return pltpu.make_async_remote_copy(
            src_ref=src, dst_ref=dst, send_sem=send.at[slot], recv_sem=recv.at[slot],
            device_id=device(i, index), device_id_type=pl.DeviceIdType.MESH,
        )

    def chunk(ref, d, m):
        n = ref.shape[0] // 3
        k = others(d).index(m)
        return ref.at[k * n : (k + 1) * n]

    first, second = {}, {}
    slot = 0
    for d, m in ((0, 1), (0, 2), (0, 3), (1, 3), (1, 2), (1, 0), (2, None)):
        src, dst = ((st, rt), (sz, rz), (sy, ry))[d]
        if m is not None:
            src, dst = chunk(src, d, m), chunk(dst, d, m)
        first[d, m] = remote(src, dst, slot, d, prv[d])
        slot += 1
    back = {}
    for m in range(4):
        n = bs.shape[0] // 4
        back[m] = remote(bs.at[m * n : (m + 1) * n], br.at[m * n : (m + 1) * n], slot, 0, nxt[0])
        slot += 1
    for i, src, dst in ((1, ezs, ezr), (2, eys, eyr)):
        back["edge", i] = pltpu.make_async_remote_copy(
            src_ref=src, dst_ref=dst, send_sem=send.at[slot], recv_sem=recv.at[slot],
            device_id=diagonal(nxt[0], i, prv[i]), device_id_type=pl.DeviceIdType.MESH,
        )
        slot += 1
    for d in (1, 2):
        src, dst = (None, (qz, pz), (qy, py))[d]
        for m in others(d):
            second[d, m] = remote(chunk(src, d, m), chunk(dst, d, m), slot, d, nxt[d])
            slot += 1

    pl.semaphore_wait(barrier, 10)
    for key, copy in first.items():
        if key[0]:
            copy.start()
    low_faces = [copy for key, copy in first.items() if not key[0]]
    high_faces = [back[key] for key in (("edge", 1), ("edge", 2), 0, 3, 2, 1)]
    around = me[0] == counts[0] - 1

    @pl.when(around)
    def _():
        for copy in high_faces + low_faces:
            copy.start()

    @pl.when(jnp.logical_not(around))
    def _():
        for copy in low_faces + high_faces:
            copy.start()

    last_rows.wait()

    def matrix(m, h):
        return [[[load(m, part, i, j, h) for j in range(3)] for i in range(3)] for part in range(2)]

    def save(ref, index, value):
        for part in range(2):
            for i in range(len(value[part])):
                for j in range(3):
                    ref[index, part, i, j] = value[part][i][j]

    def saved(ref, index, rows=3):
        return [[[ref[index, part, i, j] for j in range(3)] for i in range(rows)] for part in range(2)]

    def rolled(m, d, h, part, i, j):
        v = load(m, part, i, j, h)
        if d == 3:
            return jnp.where(g.xcol == NX - 1, g.lanes(v, NX - 1), g.lanes(v, -1))
        if d == 2:
            return g.lanes(v, -NX)
        if d == 1:
            return g.rows(v, -1)
        if h + 1 < halves:
            beyond = g.rows(load(m, part, i, j, h + 1), -depth)
            return jnp.where(g.row >= SUB - depth, beyond, g.rows(v, -depth))
        return g.rows(v, -depth)

    def complete(d, h):
        return d == 3 or (d == 0 and h + 1 < halves)

    slots = {}
    for mu, nu in PLANES:
        for h in range(halves):
            for m, d in ((nu, mu), (mu, nu)):
                slots[m, d, h] = len(slots)
                rows = 3 if complete(d, h) else 2
                save(
                    ahead_s, slots[m, d, h],
                    [[[rolled(m, d, h, part, i, j) for j in range(3)] for i in range(rows)] for part in range(2)],
                )
            save(
                local_s, PLANES.index((mu, nu)) * halves + h,
                product(matrix(mu, h), matrix(nu, h), left_h=True),
            )

    def ahead(m, d, h):
        if complete(d, h):
            return saved(ahead_s, slots[m, d, h])
        index = {c: n for n, c in enumerate(all_comps(d))}

        def get(part, i, j):
            v = ahead_s[slots[m, d, h], part, i, j]
            c = index[(m, part, i, j)]
            if d == 0:
                r = c // g.per * SUB
                edge = g.rows(rt[r : r + SUB, :], SUB - depth - depth * (c % g.per))
                return jnp.where(g.row >= SUB - depth, edge, v)
            if d == 1:
                r = (c // depth * halves + h) * SUB
                edge = g.rows(rz[r : r + SUB, :], depth - 1 - c % depth)
                return jnp.where(g.zrow == depth - 1, edge, v)
            r = (c // g.ygroups * halves + h) * SUB
            edge = g.lanes(ry[r : r + SUB, :], LANES - NX - NX * (c % g.ygroups))
            return jnp.where(g.lane >= LANES - NX, edge, v)

        real = [[get(0, i, j) for j in range(3)] for i in range(2)]
        imag = [[get(1, i, j) for j in range(3)] for i in range(2)]
        third_r, third_i = third_row(real, imag)
        return [real + [third_r], imag + [third_i]]

    seen = set()

    def add(m, c, h, value):
        r = ((m * 8 + c) * halves + h) * SUB
        if (m, c, h) in seen:
            acc[r : r + SUB, :] += value
        else:
            seen.add((m, c, h))
            acc[r : r + SUB, :] = value

    def lower(m, d, h, q):
        base = others(d).index(m) * 8
        if d == 2:
            for c0 in range(0, 8, g.ygroups):
                value = None
                for k in range(g.ygroups):
                    x = g.lanes(q[c0 + k], NX * (k + 1))
                    value = x if value is None else jnp.where(g.lane >= NX * k, x, value)
                r = ((base + c0) // g.ygroups * halves + h) * SUB
                qy[r : r + SUB, :] = value
        elif d == 1:
            for c0 in range(0, 8, depth):
                value = None
                for k in range(depth):
                    x = g.rows(q[c0 + k], k + 1 - depth)
                    value = x if value is None else jnp.where(g.zrow >= k, x, value)
                r = ((base + c0) // depth * halves + h) * SUB
                qz[r : r + SUB, :] = value
        for c in range(8):
            if d == 3:
                add(m, c, h, jnp.where(g.xcol == 0, g.lanes(q[c], 1 - NX), g.lanes(q[c], 1)))
            elif d == 2:
                add(m, c, h, jnp.where(g.lane >= NX, g.lanes(q[c], NX), 0.0))
            elif d == 1:
                add(m, c, h, jnp.where(g.zrow > 0, g.rows(q[c], 1), 0.0))
            else:
                moved = g.rows(q[c], depth)
                add(m, c, h, jnp.where(g.row >= depth, moved, 0.0))
                if h + 1 < halves:
                    add(m, c, h + 1, jnp.where(g.row < depth, moved, 0.0))

    steps = [(pair, h) for pair in PLANES if pair[0] for h in range(halves)]
    steps += [(pair, h) for h in range(halves) for pair in PLANES if not pair[0]]
    arrived, left = set(), {key: halves for key in second}
    for (mu, nu), h in steps:
        n = PLANES.index((mu, nu))
        for d, m in ((mu, nu), (nu, mu)):
            key = (d, None if d == 2 else m)
            if key in first and key not in arrived and not complete(d, h):
                arrived.add(key)
                first[key].wait_recv()
        a = product(ahead(nu, mu, h), ahead(mu, nu, h), right_h=True)
        save(plaq_s, n * halves + h, a)
        b = saved(local_s, n * halves + h)
        lower(mu, nu, h, projected(a, b, left_h=True))
        lower(nu, mu, h, projected(a, b, right_h=True))
        for key in ((mu, nu), (nu, mu)):
            if key in second:
                left[key] -= 1
                if not left[key]:
                    second[key].start()

    for n, (mu, nu) in enumerate(PLANES):
        for h in range(halves):
            e = product(matrix(mu, h), saved(plaq_s, n * halves + h))
            upper = projected(e, matrix(nu, h), right_h=True)
            for c in range(8):
                add(mu, c, h, upper[c])
                add(nu, c, h, -upper[c])

    def complete_rows(get):
        real = [[get(0, i, j) for j in range(3)] for i in range(2)]
        imag = [[get(1, i, j) for j in range(3)] for i in range(2)]
        third_r, third_i = third_row(real, imag)
        return [real + [third_r], imag + [third_i]]

    def behind(m):
        def get(part, i, j):
            c = 12 * m + part * 6 + i * 3 + j
            r = c // g.per * SUB
            return g.rows(br[r : r + SUB, :], -depth * (c % g.per))

        return complete_rows(get)

    for key in (("edge", 1), ("edge", 2), 0):
        back[key].wait_recv()
    time_link = behind(0)
    for m in (3, 2, 1):
        back[m].wait_recv()

        def step(part, i, j):
            v = time_link[part][i][j]
            c = part * 6 + i * 3 + j
            if m == 3:
                return jnp.where(g.xcol == NX - 1, g.lanes(v, NX - 1), g.lanes(v, -1))
            if m == 1:
                r = c // SUB * SUB
                edge = g.rows(ezr[r : r + SUB, :], depth - 1 - c % SUB)
                return jnp.where(g.row == depth - 1, edge, g.rows(v, -1))
            r = c // g.ygroups * SUB
            edge = g.lanes(eyr[r : r + SUB, :], LANES - NX - NX * (c % g.ygroups))
            return jnp.where(g.lane >= LANES - NX, edge, g.lanes(v, -NX))

        a = product(matrix(m, 0), complete_rows(step), right_h=True)
        b = product(time_link, behind(m), left_h=True)
        q = projected(a, b, right_h=True)
        for c in range(8):
            add(m, c, 0, jnp.where(g.row < depth, q[c], 0.0))

    for m in (3, 2, 1, 0):
        for d in others(m):
            if d in (1, 2):
                second[d, m].wait_recv()
        for h in range(halves):
            for c in range(8):
                r = ((m * 8 + c) * halves + h) * SUB
                value = acc[r : r + SUB, :]
                for d in others(m):
                    b = others(d).index(m) * 8 + c
                    if d == 1:
                        s = (b // depth * halves + h) * SUB
                        x = g.rows(pz[s : s + SUB, :], -(b % depth))
                        value = value + jnp.where(g.zrow == 0, x, 0.0)
                    elif d == 2:
                        s = (b // g.ygroups * halves + h) * SUB
                        x = g.lanes(py[s : s + SUB, :], -NX * (b % g.ygroups))
                        value = value + jnp.where(g.lane < NX, x, 0.0)
                acc[r : r + SUB, :] = value
    for copy in list(first.values()) + list(back.values()) + list(second.values()):
        copy.wait_send()


def expand(halves, acc, hbm, out, sems):
    copies = []
    for m in range(4):
        for h in range(halves):
            rows = [((m * 8 + c) * halves + h) * SUB for c in range(8)]
            f = [acc[r : r + SUB, :] * (COEFF * 0.5 if c < 6 else COEFF) for c, r in enumerate(rows)]

            def put(part, i, j, value):
                out[m, part, i, j, h * SUB : (h + 1) * SUB, :] = value

            for n, (i, j) in enumerate(((0, 1), (0, 2), (1, 2))):
                put(0, i, j, f[n])
                put(0, j, i, -f[n])
                put(1, i, j, f[3 + n])
                put(1, j, i, f[3 + n])
            for i in range(3):
                put(0, i, i, jnp.zeros((SUB, LANES), jnp.float32))
            put(1, 0, 0, f[6])
            put(1, 1, 1, f[7])
            put(1, 2, 2, -(f[6] + f[7]))
        copies.append(pltpu.make_async_copy(out.at[m], hbm.at[m], sems.at[m]))
        copies[-1].start()
    for copy in copies:
        copy.wait()


def per_device(counts, links):
    time_len, depth, flat = links.shape[4:]
    sites = time_len * depth
    assert flat == LANES and SUB % depth == 0 and sites % SUB == 0
    halves = sites // SUB
    rows1, rows2 = sizes(depth, halves)
    vmem = lambda *s: pltpu.VMEM(s + (LANES,), jnp.float32)
    shape = links.shape[:4] + (sites, flat)
    terms = pl.pallas_call(
        functools.partial(force_terms, counts, depth, halves),
        out_shape=pltpu.VMEM((32 * sites, flat), jnp.float32),
        in_specs=[pl.BlockSpec(memory_space=pl.ANY)],
        out_specs=pl.BlockSpec(memory_space=pltpu.VMEM),
        scratch_shapes=[
            vmem(*shape[:-1]),
            vmem(12 * halves, 2, 3, 3, SUB),
            vmem(6 * halves, 2, 3, 3, SUB),
            vmem(6 * halves, 2, 3, 3, SUB),
        ]
        + [vmem(r) for r in rows1 + rows1 + rows2[1:] + rows2[1:]]
        + [vmem(r) for r in (rows1[0] // 3 * 4,) * 2 + (2 * SUB,) * 4]
        + [
            pltpu.SemaphoreType.DMA((5,)),
            pltpu.SemaphoreType.DMA((19,)),
            pltpu.SemaphoreType.DMA((19,)),
        ],
        compiler_params=pltpu.CompilerParams(collective_id=0, has_side_effects=True),
        name="force_terms",
    )(links.reshape(shape))
    out = pl.pallas_call(
        functools.partial(expand, halves),
        out_shape=jax.ShapeDtypeStruct(shape, jnp.float32),
        in_specs=[pl.BlockSpec(memory_space=pltpu.VMEM)],
        out_specs=pl.BlockSpec(memory_space=pl.ANY),
        scratch_shapes=[vmem(*shape[:-1]), pltpu.SemaphoreType.DMA((4,))],
        name="expand",
    )(pltpu.with_memory_space_constraint(terms, pltpu.VMEM))
    return out.reshape(links.shape)


def solution(mesh):
    assert mesh.axis_names == ("gx", "gz", "ta")
    counts = tuple(mesh.shape[a] for a in AXES)
    spec = P(None, None, None, None, "ta", "gz", "gx")
    return jax.shard_map(
        functools.partial(per_device, counts),
        mesh=mesh,
        in_specs=(spec,),
        out_specs=spec,
        check_vma=False,
    )
```

profile of v0, /device:TPU:0, one launch (start us, length us, event | category | flops | bytes accessed | tf_op | source)
XLA Modules:
  0.0 14.3 jit_solution(12570588577540397695)
XLA Ops:
  0.0 13.4 %force_terms.1.acc = f32[512,128]{1,0:T(8,128)S(1)} custom-call(f32[4,2,3,3,16,128]{5,4,3,2,1,0:T(8,128)} %bitcast.2), custom_call_target="tpu_custom_call" | custom-call | tf_op jit(solution)/shard_map/force_terms/pallas_call | solution.py:523
  13.4 0.9 %expand.1 = f32[4,2,3,3,16,128]{5,4,3,2,1,0:T(8,128)} custom-call(f32[512,128]{1,0:T(8,128)S(1)} %force_terms.1.acc), custom_call_target="tpu_custom_call" | custom-call | tf_op jit(solution)/shard_map/expand/pallas_call | solution.py:544
where the time goes:
time: 14.4 us; the launch traced here: 14.3 us
  Pallas kernels  14.3 us (99%)
    pallas_call x1, Pallas kernels, per_device(): pl.pallas_call(functools.partial(force_terms, counts, depth, halves), out...  13.4 us
    pallas_call x1, Pallas kernels, per_device(): pl.pallas_call(functools.partial(expand, halves), out_shape=jax.ShapeDtyp...  0.86 us

commit v1 on v0

v1 whole, which is shorter than its diff:
```python
import functools

import jax
import jax.numpy as jnp
from jax import lax
from jax.experimental import pallas as pl
from jax.experimental.pallas import tpu as pltpu
from jax.sharding import PartitionSpec as P

NX = 16
COEFF = -1.9
AXES = ("ta", "gz", "gx")
SUB, LANES = 8, 128


def others(d):
    return [m for m in range(4) if m != d]


class Lattice:
    def __init__(self, depth):
        self.depth = depth
        self.per = SUB // depth
        self.ygroups = LANES // NX
        self.row = lax.broadcasted_iota(jnp.int32, (SUB, LANES), 0)
        self.lane = lax.broadcasted_iota(jnp.int32, (SUB, LANES), 1)
        self.zrow = self.row % depth
        self.xcol = self.lane % NX

    def rows(self, value, shift):
        shift %= SUB
        return pltpu.roll(value, shift, 0) if shift else value

    def lanes(self, value, shift):
        shift %= LANES
        return pltpu.roll(value, shift, 1) if shift else value


def entry(left, right, i, j, part, left_h, right_h):
    total = None
    for k in range(3):
        li = (k, i) if left_h else (i, k)
        ri = (j, k) if right_h else (k, j)
        lr, lm = left[0][li[0]][li[1]], left[1][li[0]][li[1]]
        rr, rm = right[0][ri[0]][ri[1]], right[1][ri[0]][ri[1]]
        if part == 0:
            first, second = lr * rr, lm * rm
            minus = left_h == right_h
        elif left_h:
            first, second = lr * rm, lm * rr
            minus = True
        else:
            first, second = lm * rr, lr * rm
            minus = right_h
        value = first - second if minus else first + second
        total = value if total is None else total + value
    return total


def product(left, right, left_h=False, right_h=False):
    return [
        [[entry(left, right, i, j, part, left_h, right_h) for j in range(3)] for i in range(3)]
        for part in range(2)
    ]


def projected(left, right, left_h=False, right_h=False):
    get = lambda i, j, part: entry(left, right, i, j, part, left_h, right_h)
    pairs = ((0, 1), (0, 2), (1, 2))
    real = [get(i, j, 0) - get(j, i, 0) for i, j in pairs]
    imag = [get(i, j, 1) + get(j, i, 1) for i, j in pairs]
    diag = [get(i, i, 1) for i in range(3)]
    third = (diag[0] + diag[1] + diag[2]) * (1.0 / 3.0)
    return real + imag + [diag[0] - third, diag[1] - third]


def third_row(real, imag):
    rows_r, rows_i = [], []
    for column in range(3):
        n, l = (column + 1) % 3, (column + 2) % 3
        rows_r.append(
            real[0][n] * real[1][l]
            - imag[0][n] * imag[1][l]
            - real[0][l] * real[1][n]
            + imag[0][l] * imag[1][n]
        )
        rows_i.append(
            real[0][l] * imag[1][n]
            + imag[0][l] * real[1][n]
            - real[0][n] * imag[1][l]
            - imag[0][n] * real[1][l]
        )
    return rows_r, rows_i


PLANES = ((2, 3), (1, 3), (1, 2), (0, 1), (0, 2), (0, 3))
KINDS = ({0: 1}, {1: 1}, {2: 1}, {0: 1, 1: -1}, {0: 1, 2: -1}, {1: 1, 2: -1})
CORNERS = {(0, 1): (3, 1), (1, 0): (3, -1), (0, 2): (4, 1), (2, 0): (4, -1), (1, 2): (5, 1), (2, 1): (5, -1)}
FIXED = [(0, 1, 0), (0, 2, 0), (1, 0, -1), (1, 2, None), (2, 0, -1), (2, 1, None)]


def force_terms(
    counts, depth, halves, hbm, acc,
    u, ahead_s, local_s, fixed_s, st, sz, sy, rt, rz, ry, vts, vzs, vys, vtr, vzr, vyr,
    c01, c10, c02, c20, c12, c21, k01, k10, k02, k20, k12, k21,
    load_sem, send, recv, ready,
):
    g = Lattice(depth)
    last = halves - 1
    me = [lax.axis_index(a) for a in AXES]
    corner_out = {(0, 1): c01, (1, 0): c10, (0, 2): c02, (2, 0): c20, (1, 2): c12, (2, 1): c21}
    corner_in = {(0, 1): k01, (1, 0): k10, (0, 2): k02, (2, 0): k20, (1, 2): k12, (2, 1): k21}

    loads = [
        pltpu.make_async_copy(hbm.at[m, :, 0:2], u.at[m, :, 0:2], load_sem.at[m]) for m in range(4)
    ]
    last_rows = pltpu.make_async_copy(hbm.at[:, :, 2], u.at[:, :, 2], load_sem.at[4])
    for m in (0, 3, 1, 2):
        loads[m].start()
    last_rows.start()

    def peer(kind, sign):
        where = list(me)
        for i, step in KINDS[kind].items():
            where[i] = lax.rem(me[i] + counts[i] + sign * step, counts[i])
        by = dict(zip(AXES, where))
        return (by["gx"], by["gz"], by["ta"])

    def axis_of(kind):
        return next(iter(KINDS[kind]))

    def greets(axis, sign):
        return me[axis] < counts[axis] - 1 if sign > 0 else me[axis] == 0

    barrier = pltpu.get_barrier_semaphore()
    expected = 0
    for axis in range(3):
        for sign in (1, -1):
            kinds = [k for k in range(6) if axis_of(k) == axis]
            expected = expected + jnp.where(greets(axis, sign), 0, len(kinds))

            @pl.when(greets(axis, sign))
            def _():
                for k in kinds:
                    pl.semaphore_signal(
                        barrier, inc=1, device_id=peer(k, sign), device_id_type=pl.DeviceIdType.MESH
                    )

    @pl.when(expected > 0)
    def _():
        pl.semaphore_wait(barrier, expected)

    for axis in range(3):
        for sign in (1, -1):
            kinds = [k for k in range(6) if axis_of(k) == axis]

            @pl.when(jnp.logical_not(greets(axis, sign)))
            def _():
                for k in kinds:
                    pl.semaphore_signal(
                        ready.at[2 * k + (sign > 0)], inc=1,
                        device_id=peer(k, sign), device_id_type=pl.DeviceIdType.MESH,
                    )

    def met(kind, sign):
        pl.semaphore_wait(ready.at[2 * kind + (sign < 0)], 1)

    def meet(kind, sign):
        @pl.when(greets(axis_of(kind), sign))
        def _():
            met(kind, sign)

    def load(m, part, i, j, h):
        return u[m, part, i, j, h * SUB : (h + 1) * SUB, :]

    COMPS = [(part, i, j) for part in range(2) for i in range(2) for j in range(3)]

    def comps(m):
        return [(m,) + c for c in COMPS]

    def all_comps(d):
        return [c for m in others(d) for c in comps(m)]

    def flat(value):
        return [value[part][i][j] for part, i, j in COMPS]

    def merge(values, index, step):
        total = None
        for k, x in enumerate(values):
            total = x if total is None else jnp.where(index >= step * k, x, total)
        return total

    def pack_t(m):
        cs, base = comps(m), 12 * others(0).index(m)
        for c0 in range(0, 12, g.per):
            r = (base + c0) // g.per * SUB
            st[r : r + SUB, :] = merge(
                [g.rows(load(*cs[c0 + k], 0), depth * k) for k in range(g.per)], g.row, depth
            )

    def pack_z(m):
        cs, base = comps(m), 12 * others(1).index(m)
        for c0 in range(0, 12, depth):
            for h in range(halves):
                r = ((base + c0) // depth * halves + h) * SUB
                sz[r : r + SUB, :] = merge(
                    [g.rows(load(*cs[c0 + k], h), k) for k in range(depth)], g.zrow, 1
                )

    def pack_y():
        cs = all_comps(2)
        for c0 in range(0, len(cs), g.ygroups):
            for h in range(halves):
                r = (c0 // g.ygroups * halves + h) * SUB
                sy[r : r + SUB, :] = merge(
                    [
                        g.lanes(load(*cs[c0 + k], h), NX * k)
                        for k in range(min(g.ygroups, len(cs) - c0))
                    ],
                    g.lane, NX,
                )

    def pack_vt(m, v):
        base = 12 * others(0).index(m)
        for c0 in range(0, 12, g.per):
            r = (base + c0) // g.per * SUB
            vts[r : r + SUB, :] = merge(
                [g.rows(v[c0 + k], depth * (k + 1)) for k in range(g.per)], g.row, depth
            )

    def pack_vz(m, h, v):
        base = 12 * others(1).index(m)
        for c0 in range(0, 12, depth):
            r = ((base + c0) // depth * halves + h) * SUB
            vzs[r : r + SUB, :] = merge(
                [g.rows(v[c0 + k], k + 1 - depth) for k in range(depth)], g.zrow, 1
            )

    def pack_vy(m, v):
        n = vys.shape[0] // 3
        for c0 in range(0, 12 * halves, g.ygroups):
            r = others(2).index(m) * n + c0 // g.ygroups * SUB
            vys[r : r + SUB, :] = merge(
                [
                    g.lanes(v[c0 + k], NX * (k + 1))
                    for k in range(min(g.ygroups, 12 * halves - c0))
                ],
                g.lane, NX,
            )

    def by_groups(d, h, up, shift, index, step):
        cs = comps(d)
        return merge(
            [
                merge(
                    [
                        g.lanes(g.rows(load(*cs[c], h), shift(c // g.ygroups)), NX * (c % g.ygroups + up))
                        for c in range(c0, min(12, c0 + g.ygroups))
                    ],
                    g.lane, NX,
                )
                for c0 in range(0, 12, g.ygroups)
            ],
            index, step,
        )

    def pack_corner(d, m):
        ref, cs = corner_out[d, m], comps(d)
        if (d, m) in ((0, 1), (1, 0)):
            source = SUB - depth if d == 0 else depth - 1
            for c0 in range(0, 12, SUB):
                ref[c0 : c0 + SUB, :] = merge(
                    [
                        g.rows(load(*cs[c0 + k], last if d == 0 else 0), k - source)
                        for k in range(min(SUB, 12 - c0))
                    ],
                    g.row, 1,
                )
        elif (d, m) == (0, 2):
            ref[...] = by_groups(0, last, 0, lambda k: depth * (k + 1), g.row, depth)
        elif (d, m) == (2, 0):
            ref[...] = by_groups(2, 0, 1, lambda k: depth * k, g.row, depth)
        else:
            for h in range(halves):
                up, source = (0, depth - 1) if d == 1 else (1, 0)
                ref[h * SUB : (h + 1) * SUB, :] = by_groups(
                    d, h, up, lambda k: k - source, g.zrow, 1
                )

    def corner(d, m, h, c):
        ref = corner_in[d, m]
        k, group = c // g.ygroups, NX * (c % g.ygroups)
        if (d, m) in ((0, 1), (1, 0)):
            target = depth - 1 if d == 0 else SUB - depth
            r = c // SUB * SUB
            return g.rows(ref[r : r + SUB, :], target - c % SUB)
        if (d, m) == (0, 2):
            return g.lanes(g.rows(ref[...], -depth * k), LANES - NX - group)
        if (d, m) == (2, 0):
            return g.lanes(g.rows(ref[...], SUB - depth - depth * k), -group)
        value = ref[h * SUB : (h + 1) * SUB, :]
        if d == 1:
            return g.lanes(g.rows(value, -k), LANES - NX - group)
        return g.lanes(g.rows(value, depth - 1 - k), -group)

    slots = {}

    def remote(src, dst, kind, sign):
        slot = len(slots)
        slots[slot] = pltpu.make_async_remote_copy(
            src_ref=src, dst_ref=dst, send_sem=send.at[slot], recv_sem=recv.at[slot],
            device_id=peer(kind, sign), device_id_type=pl.DeviceIdType.MESH,
        )
        return slots[slot]

    def chunk(ref, d, m):
        n = ref.shape[0] // 3
        k = others(d).index(m)
        return ref.at[k * n : (k + 1) * n]

    low = {
        (d, m): remote(chunk(s, d, m), chunk(r, d, m), d, -1)
        for d, s, r in ((0, st, rt), (1, sz, rz)) for m in others(d)
    }
    low[2, None] = remote(sy, ry, 2, -1)
    high = {
        (d, m): remote(chunk(s, d, m), chunk(r, d, m), d, 1)
        for d, s, r in ((0, vts, vtr), (1, vzs, vzr), (2, vys, vyr)) for m in others(d)
    }
    corners = {
        key: remote(corner_out[key], corner_in[key], kind, sign)
        for key, (kind, sign) in CORNERS.items()
    }

    def matrix(m, h):
        return [[[load(m, part, i, j, h) for j in range(3)] for i in range(3)] for part in range(2)]

    def save(ref, index, value):
        for part in range(2):
            for i in range(len(value[part])):
                for j in range(3):
                    ref[index, part, i, j] = value[part][i][j]

    def saved(ref, index, rows=3):
        return [[[ref[index, part, i, j] for j in range(3)] for i in range(rows)] for part in range(2)]

    def rolled(m, d, h, part, i, j):
        v = load(m, part, i, j, h)
        if d == 3:
            return jnp.where(g.xcol == NX - 1, g.lanes(v, NX - 1), g.lanes(v, -1))
        if d == 2:
            return g.lanes(v, -NX)
        if d == 1:
            return g.rows(v, -1)
        if h + 1 < halves:
            beyond = g.rows(load(m, part, i, j, h + 1), -depth)
            return jnp.where(g.row >= SUB - depth, beyond, g.rows(v, -depth))
        return g.rows(v, -depth)

    def complete(d, h):
        return d == 3 or (d == 0 and h + 1 < halves)

    def far_edge(d):
        return (g.row >= SUB - depth, g.zrow == depth - 1, g.lane >= LANES - NX)[d]

    ahead_slot = {}

    def prepare(m, d, h, rows):
        value = [
            [[rolled(m, d, h, part, i, j) for j in range(3)] for i in range(3 if rows == 3 or complete(d, h) else 2)]
            for part in range(2)
        ]
        ahead_slot[m, d, h] = len(ahead_slot)
        keep = 3 if complete(d, h) else 2
        save(ahead_s, ahead_slot[m, d, h], [part[:keep] for part in value])
        return value

    def transported(b, m, d, h, b_h):
        moved = prepare(m, d, h, 3)
        value = [
            [[entry(b, moved, i, j, part, b_h, False) for j in range(3)] for i in range(2)]
            for part in range(2)
        ]
        if not complete(d, h):
            edge = far_edge(d)
            for part in range(2):
                for i in range(2):
                    for j in range(3):
                        own = b[part][j][i] if b_h else b[part][i][j]
                        own = -own if b_h and part else own
                        value[part][i][j] = jnp.where(edge, own, value[part][i][j])
        return flat(value)

    local = {}

    def local_product(mu, nu, h):
        b = product(matrix(mu, h), matrix(nu, h), left_h=True)
        save(local_s, PLANES.index((mu, nu)) * halves + h, b)
        return b

    for copy in [loads[m] for m in (0, 3, 1, 2)] + [last_rows]:
        copy.wait()
    pack_corner(0, 1)
    pack_corner(0, 2)
    for m in (3, 1, 2):
        b = local_product(0, m, last)
        pack_vt(m, transported(b, 0, m, last, False))

    at_end = me[0] == counts[0] - 1
    upward = [corners[0, 1], corners[0, 2]] + [high[0, m] for m in (3, 1, 2)]
    downward = [low[0, m] for m in (3, 1, 2)] + [corners[1, 0], corners[2, 0]]

    @pl.when(at_end)
    def _():
        for copy in upward:
            copy.start()

    pack_y()
    meet(2, -1)
    low[2, None].start()
    for m in (3, 2, 0):
        pack_z(m)
    pack_corner(1, 2)
    pack_corner(2, 1)
    meet(1, -1)
    for m in (3, 2, 0):
        low[1, m].start()
    meet(5, 1)
    corners[1, 2].start()
    meet(5, -1)
    corners[2, 1].start()
    for m in (3, 1, 2):
        pack_t(m)
    pack_corner(1, 0)
    pack_corner(2, 0)

    @pl.when(me[0] > 0)
    def _():
        for copy in downward:
            copy.start()

    @pl.when(jnp.logical_not(at_end))
    def _():
        for kind in (0, 3, 4):
            met(kind, 1)
        for copy in upward:
            copy.start()

    for mu, nu in ((2, 3), (1, 3), (1, 2), (0, 2), (0, 1), (0, 3)):
        lifted = {}
        for h in range(halves):
            if mu == 0 and h == last:
                b = saved(local_s, PLANES.index((mu, nu)) * halves + h)
            else:
                b = local_product(mu, nu, h)
            if mu:
                lifted[mu, nu, h] = transported(b, mu, nu, h, False)
            elif h != last:
                prepare(mu, nu, h, 2)
            if nu != 3:
                lifted[nu, mu, h] = transported(b, nu, mu, h, True)
            else:
                prepare(nu, mu, h, 2)
        for d, m in ((mu, nu), (nu, mu)):
            if d == 1:
                for h in range(halves):
                    pack_vz(m, h, lifted[d, m, h])
            elif d == 2:
                pack_vy(m, [x for h in range(halves) for x in lifted[d, m, h]])
            if d in (1, 2):
                if (d, m) in ((2, 3), (1, 3)):
                    meet(d, 1)
                high[d, m].start()

    def ahead(m, d, h):
        if complete(d, h):
            return saved(ahead_s, ahead_slot[m, d, h])
        index = {c: n for n, c in enumerate(all_comps(d))}

        def get(part, i, j):
            v = ahead_s[ahead_slot[m, d, h], part, i, j]
            c = index[(m, part, i, j)]
            if d == 0:
                r = c // g.per * SUB
                edge = g.rows(rt[r : r + SUB, :], SUB - depth - depth * (c % g.per))
            elif d == 1:
                r = (c // depth * halves + h) * SUB
                edge = g.rows(rz[r : r + SUB, :], depth - 1 - c % depth)
            else:
                r = (c // g.ygroups * halves + h) * SUB
                edge = g.lanes(ry[r : r + SUB, :], LANES - NX - NX * (c % g.ygroups))
            return jnp.where(far_edge(d), edge, v)

        return complete_rows(get)

    def complete_rows(get):
        real = [[get(0, i, j) for j in range(3)] for i in range(2)]
        imag = [[get(1, i, j) for j in range(3)] for i in range(2)]
        third_r, third_i = third_row(real, imag)
        return [real + [third_r], imag + [third_i]]

    seen = set()

    def add(m, c, h, value):
        r = ((m * 8 + c) * halves + h) * SUB
        if (m, c, h) in seen:
            acc[r : r + SUB, :] += value
        else:
            seen.add((m, c, h))
            acc[r : r + SUB, :] = value

    def shifted(q, d):
        if d == 3:
            return jnp.where(g.xcol == 0, g.lanes(q, 1 - NX), g.lanes(q, 1))
        if d == 2:
            return jnp.where(g.lane >= NX, g.lanes(q, NX), 0.0)
        if d == 1:
            return jnp.where(g.zrow > 0, g.rows(q, 1), 0.0)
        return jnp.where(g.row >= depth, g.rows(q, depth), 0.0)

    def plane(mu, nu, h):
        a = product(ahead(nu, mu, h), ahead(mu, nu, h), right_h=True)
        b = saved(local_s, PLANES.index((mu, nu)) * halves + h)
        e = product(matrix(mu, h), a)
        upper = projected(e, matrix(nu, h), right_h=True)
        q = projected(a, b, left_h=True)
        for c in range(8):
            add(mu, c, h, shifted(q[c], nu) + upper[c])
        q = projected(a, b, right_h=True)
        for c in range(8):
            add(nu, c, h, shifted(q[c], mu) - upper[c])
            if mu == 0 and h + 1 < halves:
                add(nu, c, h + 1, jnp.where(g.row < depth, g.rows(q[c], depth), 0.0))

    fixed_slot = {}

    def fix(d, m, h):
        beyond = complete_rows(lambda part, i, j: corner(d, m, h, part * 6 + i * 3 + j))
        own = matrix(m, h)
        moved = product(own, beyond, right_h=True)
        edge = far_edge(m)
        fixed_slot[d, m, h] = len(fixed_slot)
        save(
            fixed_s, fixed_slot[d, m, h],
            [[[jnp.where(edge, moved[p][i][j], own[p][i][j]) for j in range(3)] for i in range(3)] for p in range(2)],
        )

    def lower(d, m, h):
        def get(part, i, j):
            c = part * 6 + i * 3 + j
            base = 12 * others(d).index(m) + c
            if d == 0:
                r = base // g.per * SUB
                return g.rows(vtr[r : r + SUB, :], -depth * (base % g.per))
            if d == 1:
                r = (base // depth * halves + h) * SUB
                return g.rows(vzr[r : r + SUB, :], -(base % depth))
            n, k = vyr.shape[0] // 3, h * 12 + c
            r = others(2).index(m) * n + k // g.ygroups * SUB
            return g.lanes(vyr[r : r + SUB, :], -NX * (k % g.ygroups))

        if (d, m, h) in fixed_slot:
            left = saved(fixed_s, fixed_slot[d, m, h])
        else:
            left = matrix(m, h)
        q = projected(left, complete_rows(get), right_h=True)
        near = (g.row < depth, g.zrow == 0, g.lane < NX)[d]
        for c in range(8):
            add(m, c, h, jnp.where(near, q[c], 0.0))

    for h in range(last):
        plane(0, 3, h)
    low[2, None].wait_recv()
    for h in range(halves):
        plane(2, 3, h)
    for h in range(last):
        plane(0, 2, h)
    low[1, 3].wait_recv()
    for h in range(halves):
        plane(1, 3, h)
    low[1, 2].wait_recv()
    for h in range(halves):
        plane(1, 2, h)
    low[1, 0].wait_recv()
    for h in range(last):
        plane(0, 1, h)

    @pl.when(me[0] == 0)
    def _():
        for kind in (0, 3, 4):
            met(kind, -1)
        for copy in downward:
            copy.start()

    for d, m in ((2, 3), (2, 1), (2, 0), (1, 3), (1, 2), (1, 0)):
        if (d, m) in ((2, 1), (1, 2)):
            corners[d, m].wait_recv()
            for h in range(halves):
                fix(d, m, h)
        high[d, m].wait_recv()
        for h in range(halves if m else last):
            lower(d, m, h)
    for m in (3, 1, 2):
        low[0, m].wait_recv()
        plane(0, m, last)
    for d in (1, 2):
        corners[d, 0].wait_recv()
        fix(d, 0, last)
        lower(d, 0, last)
    for m in (1, 2):
        corners[0, m].wait_recv()
        fix(0, m, 0)
    for m in (3, 1, 2):
        high[0, m].wait_recv()
        lower(0, m, 0)
    for copy in slots.values():
        copy.wait_send()


def expand(halves, acc, hbm, out, sems):
    copies = []
    for m in range(4):
        for h in range(halves):
            rows = [((m * 8 + c) * halves + h) * SUB for c in range(8)]
            f = [acc[r : r + SUB, :] * (COEFF * 0.5 if c < 6 else COEFF) for c, r in enumerate(rows)]

            def put(part, i, j, value):
                out[m, part, i, j, h * SUB : (h + 1) * SUB, :] = value

            for n, (i, j) in enumerate(((0, 1), (0, 2), (1, 2))):
                put(0, i, j, f[n])
                put(0, j, i, -f[n])
                put(1, i, j, f[3 + n])
                put(1, j, i, f[3 + n])
            for i in range(3):
                put(0, i, i, jnp.zeros((SUB, LANES), jnp.float32))
            put(1, 0, 0, f[6])
            put(1, 1, 1, f[7])
            put(1, 2, 2, -(f[6] + f[7]))
        copies.append(pltpu.make_async_copy(out.at[m], hbm.at[m], sems.at[m]))
        copies[-1].start()
    for copy in copies:
        copy.wait()


def per_device(counts, links):
    time_len, depth, flat = links.shape[4:]
    sites = time_len * depth
    assert flat == LANES and SUB % depth == 0 and sites % SUB == 0 and 2 <= depth <= SUB // 2
    halves = sites // SUB
    per, yg = SUB // depth, LANES // NX
    up = lambda a, b: -(-a // b) * SUB
    vmem = lambda *s: pltpu.VMEM(s + (LANES,), jnp.float32)
    shape = links.shape[:4] + (sites, flat)
    rt, rz, ry = up(36, per), up(36, depth) * halves, up(36, yg) * halves
    vy = 3 * up(12 * halves, yg)
    corner = [vmem(r) for r in (2 * SUB, 2 * SUB, SUB, SUB, SUB * halves, SUB * halves)]
    terms = pl.pallas_call(
        functools.partial(force_terms, counts, depth, halves),
        out_shape=pltpu.VMEM((32 * sites, flat), jnp.float32),
        in_specs=[pl.BlockSpec(memory_space=pl.ANY)],
        out_specs=pl.BlockSpec(memory_space=pltpu.VMEM),
        scratch_shapes=[
            vmem(*shape[:-1]),
            vmem(12 * halves, 2, 3, 3, SUB),
            vmem(6 * halves, 2, 3, 3, SUB),
            vmem(4 + 2 * halves, 2, 3, 3, SUB),
        ]
        + [vmem(r) for r in (rt, rz, ry) * 2 + (rt, rz, vy) * 2]
        + corner * 2
        + [
            pltpu.SemaphoreType.DMA((5,)),
            pltpu.SemaphoreType.DMA((22,)),
            pltpu.SemaphoreType.DMA((22,)),
            pltpu.SemaphoreType.REGULAR((12,)),
        ],
        compiler_params=pltpu.CompilerParams(collective_id=0, has_side_effects=True),
        name="force_terms",
    )(links.reshape(shape))
    out = pl.pallas_call(
        functools.partial(expand, halves),
        out_shape=jax.ShapeDtypeStruct(shape, jnp.float32),
        in_specs=[pl.BlockSpec(memory_space=pltpu.VMEM)],
        out_specs=pl.BlockSpec(memory_space=pl.ANY),
        scratch_shapes=[vmem(*shape[:-1]), pltpu.SemaphoreType.DMA((4,))],
        name="expand",
    )(pltpu.with_memory_space_constraint(terms, pltpu.VMEM))
    return out.reshape(links.shape)


def solution(mesh):
    assert mesh.axis_names == ("gx", "gz", "ta")
    counts = tuple(mesh.shape[a] for a in AXES)
    spec = P(None, None, None, None, "ta", "gz", "gx")
    return jax.shard_map(
        functools.partial(per_device, counts),
        mesh=mesh,
        in_specs=(spec,),
        out_specs=spec,
        check_vma=False,
    )
```

time: 14.4 us -> 13 us (0.903)
  Pallas kernels: 14.3 us -> 12.8 us
    pallas_call x1, Pallas kernels: 13.4 us -> 12 us  [per_device(): pl.pallas_call(functools.partial(force_terms, counts, depth, halves), out...]
where the time goes in v1:
time: 13 us; the launch traced here: 12.8 us
  Pallas kernels  12.8 us (98%)
    pallas_call x1, Pallas kernels, per_device(): pl.pallas_call(functools.partial(force_terms, counts, depth, halves), out...  12 us
    pallas_call x1, Pallas kernels, per_device(): pl.pallas_call(functools.partial(expand, halves), out_shape=jax.ShapeDtyp...  0.86 us

profile of v1, /device:TPU:0, one launch (start us, length us, event | category | flops | bytes accessed | tf_op | source)
XLA Modules:
  0.0 12.8 jit_solution(201714590866926404)
XLA Ops:
  0.0 12.0 %force_terms.1.acc = f32[512,128]{1,0:T(8,128)S(1)} custom-call(f32[4,2,3,3,16,128]{5,4,3,2,1,0:T(8,128)} %bitcast.2), custom_call_target="tpu_custom_call" | custom-call | tf_op jit(solution)/shard_map/force_terms/pallas_call | solution.py:658
  12.0 0.9 %expand.1 = f32[4,2,3,3,16,128]{5,4,3,2,1,0:T(8,128)} custom-call(f32[512,128]{1,0:T(8,128)S(1)} %force_terms.1.acc), custom_call_target="tpu_custom_call" | custom-call | tf_op jit(solution)/shard_map/expand/pallas_call | solution.py:680

commit v2 on v1

--- a/solution.py
+++ b/solution.py
@@ -126,49 +126,54 @@
         by = dict(zip(AXES, where))
         return (by["gx"], by["gz"], by["ta"])
 
-    def axis_of(kind):
-        return next(iter(KINDS[kind]))
-
-    def greets(axis, sign):
+    def above(axis, sign):
         return me[axis] < counts[axis] - 1 if sign > 0 else me[axis] == 0
 
+    def lowest(kind, sign):
+        tests = [above(i, sign * step) for i, step in KINDS[kind].items()]
+        return functools.reduce(jnp.logical_and, tests)
+
+    def highest(kind, sign):
+        tests = [above(i, sign * step) for i, step in KINDS[kind].items()]
+        return jnp.logical_not(functools.reduce(jnp.logical_or, tests))
+
     barrier = pltpu.get_barrier_semaphore()
+    pairs = [(kind, sign) for kind in range(6) for sign in (1, -1)]
     expected = 0
-    for axis in range(3):
-        for sign in (1, -1):
-            kinds = [k for k in range(6) if axis_of(k) == axis]
-            expected = expected + jnp.where(greets(axis, sign), 0, len(kinds))
-
-            @pl.when(greets(axis, sign))
-            def _():
-                for k in kinds:
-                    pl.semaphore_signal(
-                        barrier, inc=1, device_id=peer(k, sign), device_id_type=pl.DeviceIdType.MESH
-                    )
+    for kind, sign in pairs:
+        expected = expected + jnp.where(highest(kind, sign), 1, 0)
+
+        @pl.when(lowest(kind, sign))
+        def _():
+            pl.semaphore_signal(
+                barrier, inc=1, device_id=peer(kind, sign), device_id_type=pl.DeviceIdType.MESH
+            )
 
     @pl.when(expected > 0)
     def _():
         pl.semaphore_wait(barrier, expected)
 
-    for axis in range(3):
-        for sign in (1, -1):
-            kinds = [k for k in range(6) if axis_of(k) == axis]
-
-            @pl.when(jnp.logical_not(greets(axis, sign)))
-            def _():
-                for k in kinds:
-                    pl.semaphore_signal(
-                        ready.at[2 * k + (sign > 0)], inc=1,
-                        device_id=peer(k, sign), device_id_type=pl.DeviceIdType.MESH,
-                    )
-
-    def met(kind, sign):
-        pl.semaphore_wait(ready.at[2 * kind + (sign < 0)], 1)
-
-    def meet(kind, sign):
-        @pl.when(greets(axis_of(kind), sign))
+    for kind, sign in pairs:
+
+        @pl.when(highest(kind, sign))
         def _():
-            met(kind, sign)
+            pl.semaphore_signal(
+                ready.at[2 * kind + (sign > 0)], inc=1,
+                device_id=peer(kind, sign), device_id_type=pl.DeviceIdType.MESH,
+            )
+
+    def early(kind, sign, copies):
+        @pl.when(highest(kind, sign))
+        def _():
+            for copy in copies:
+                copy.start()
+
+    def late(kind, sign, copies):
+        @pl.when(lowest(kind, sign))
+        def _():
+            pl.semaphore_wait(ready.at[2 * kind + (sign < 0)], 1)
+            for copy in copies:
+                copy.start()
 
     def load(m, part, i, j, h):
         return u[m, part, i, j, h * SUB : (h + 1) * SUB, :]
@@ -406,48 +411,28 @@
         b = local_product(0, m, last)
         pack_vt(m, transported(b, 0, m, last, False))
 
-    at_end = me[0] == counts[0] - 1
-    upward = [corners[0, 1], corners[0, 2]] + [high[0, m] for m in (3, 1, 2)]
-    downward = [low[0, m] for m in (3, 1, 2)] + [corners[1, 0], corners[2, 0]]
-
-    @pl.when(at_end)
-    def _():
-        for copy in upward:
-            copy.start()
-
-    pack_y()
-    meet(2, -1)
-    low[2, None].start()
+    above_t, below_t = [high[0, m] for m in (3, 1, 2)], [low[0, m] for m in (3, 1, 2)]
+    above_z, below_z = [high[1, m] for m in (3, 0, 2)], [low[1, m] for m in (3, 2, 0)]
+    above_y, below_y = [high[2, m] for m in (3, 0, 1)], [low[2, None]]
+    for d in (1, 2):
+        early(*CORNERS[0, d], [corners[0, d]])
+    early(0, 1, above_t)
+    for m in (3, 1, 2):
+        pack_t(m)
+    early(0, -1, below_t)
     for m in (3, 2, 0):
         pack_z(m)
-    pack_corner(1, 2)
-    pack_corner(2, 1)
-    meet(1, -1)
-    for m in (3, 2, 0):
-        low[1, m].start()
-    meet(5, 1)
-    corners[1, 2].start()
-    meet(5, -1)
-    corners[2, 1].start()
-    for m in (3, 1, 2):
-        pack_t(m)
-    pack_corner(1, 0)
-    pack_corner(2, 0)
-
-    @pl.when(me[0] > 0)
-    def _():
-        for copy in downward:
-            copy.start()
-
-    @pl.when(jnp.logical_not(at_end))
-    def _():
-        for kind in (0, 3, 4):
-            met(kind, 1)
-        for copy in upward:
-            copy.start()
-
-    for mu, nu in ((2, 3), (1, 3), (1, 2), (0, 2), (0, 1), (0, 3)):
-        lifted = {}
+    early(1, -1, below_z)
+    pack_y()
+    early(2, -1, below_y)
+    for key in ((1, 0), (2, 0), (1, 2), (2, 1)):
+        pack_corner(*key)
+    for key in ((1, 0), (2, 0), (1, 2), (2, 1)):
+        early(*CORNERS[key], [corners[key]])
+
+    lifted = {}
+
+    def lift(mu, nu):
         for h in range(halves):
             if mu == 0 and h == last:
                 b = saved(local_s, PLANES.index((mu, nu)) * halves + h)
@@ -467,10 +452,32 @@
                     pack_vz(m, h, lifted[d, m, h])
             elif d == 2:
                 pack_vy(m, [x for h in range(halves) for x in lifted[d, m, h]])
-            if d in (1, 2):
-                if (d, m) in ((2, 3), (1, 3)):
-                    meet(d, 1)
-                high[d, m].start()
+
+    lift(1, 3)
+    lift(0, 1)
+    lift(1, 2)
+    early(1, 1, above_z)
+    late(1, -1, below_z)
+    late(0, 1, above_t)
+    late(2, -1, below_y)
+    late(1, 1, above_z)
+    lift(2, 3)
+    lift(0, 2)
+    early(2, 1, above_y)
+    late(2, 1, above_y)
+    lift(0, 3)
+    for key in ((0, 1), (0, 2), (1, 2), (2, 1)):
+        late(*CORNERS[key], [corners[key]])
+
+        @pl.when(jnp.logical_not(jnp.logical_or(lowest(*CORNERS[key]), highest(*CORNERS[key]))))
+        def _():
+            corners[key].start()
+
+    for key in ((1, 0), (2, 0)):
+
+        @pl.when(jnp.logical_and(me[0] > 0, jnp.logical_not(highest(*CORNERS[key]))))
+        def _():
+            corners[key].start()
 
     def ahead(m, d, h):
         if complete(d, h):
@@ -575,6 +582,14 @@
         plane(2, 3, h)
     for h in range(last):
         plane(0, 2, h)
+    late(0, -1, below_t)
+    for key in ((1, 0), (2, 0)):
+        late(*CORNERS[key], [corners[key]])
+
+        @pl.when(jnp.logical_and(me[0] == 0, jnp.logical_not(lowest(*CORNERS[key]))))
+        def _():
+            corners[key].start()
+
     low[1, 3].wait_recv()
     for h in range(halves):
         plane(1, 3, h)
@@ -584,13 +599,6 @@
     low[1, 0].wait_recv()
     for h in range(last):
         plane(0, 1, h)
-
-    @pl.when(me[0] == 0)
-    def _():
-        for kind in (0, 3, 4):
-            met(kind, -1)
-        for copy in downward:
-            copy.start()
 
     for d, m in ((2, 3), (2, 1), (2, 0), (1, 3), (1, 2), (1, 0)):
         if (d, m) in ((2, 1), (1, 2)):

time: 13 us -> 11.7 us (0.90)
  the two profiles are of different devices: /device:TPU:0 before, /device:TPU:1 now
where the time goes in v2:
time: 11.7 us; the launch traced here: 11.6 us
  Pallas kernels  11.6 us (99%)
    pallas_call x1, Pallas kernels, per_device(): pl.pallas_call(functools.partial(force_terms, counts, depth, halves), out...  10.7 us
    pallas_call x1, Pallas kernels, per_device(): pl.pallas_call(functools.partial(expand, halves), out_shape=jax.ShapeDtyp...  0.86 us

profile of v2, /device:TPU:1, one launch (start us, length us, event | category | flops | bytes accessed | tf_op | source)
XLA Modules:
  0.0 11.6 jit_solution(5764445920812139826)
XLA Ops:
  0.0 10.7 %force_terms.1.acc = f32[512,128]{1,0:T(8,128)S(1)} custom-call(f32[4,2,3,3,16,128]{5,4,3,2,1,0:T(8,128)} %bitcast.2), custom_call_target="tpu_custom_call" | custom-call | tf_op jit(solution)/shard_map/force_terms/pallas_call | solution.py:666
  10.7 0.9 %expand.1 = f32[4,2,3,3,16,128]{5,4,3,2,1,0:T(8,128)} custom-call(f32[512,128]{1,0:T(8,128)S(1)} %force_terms.1.acc), custom_call_target="tpu_custom_call" | custom-call | tf_op jit(solution)/shard_map/expand/pallas_call | solution.py:688

commit v3 on v2

--- a/solution.py
+++ b/solution.py
@@ -99,24 +99,47 @@
 FIXED = [(0, 1, 0), (0, 2, 0), (1, 0, -1), (1, 2, None), (2, 0, -1), (2, 1, None)]
 
 
+def mail(depth, halves):
+    up = lambda a, b: -(-a // b) * SUB
+    per, yg = SUB // depth, LANES // NX
+    t, z, y = up(12, per), up(12, depth) * halves, up(36, yg) * halves
+    groups = (
+        ((("low", 2), y),),
+        ((("low", 1, 3), z),),
+        ((("low", 1, 0), z),),
+        ((("low", 1, 2), z),),
+        ((("high", 2), 3 * up(12 * halves, yg)), ((2, 1), SUB * halves)),
+        ((("high", 1, 3), z), (("high", 1, 0), z)),
+        ((("high", 1, 2), z), ((1, 2), SUB * halves)),
+        ((("low", 0, 3), t),),
+        ((("low", 0, 1), t), (("low", 0, 2), t)),
+        (((1, 0), 2 * SUB), ((2, 0), SUB)),
+        ((("high", 0, 3), t), ((0, 1), 2 * SUB), ((0, 2), SUB)),
+        ((("high", 0, 1), t),),
+        ((("high", 0, 2), t),),
+    )
+    places, spans, row = {}, [], 0
+    for group in groups:
+        first = row
+        for name, rows in group:
+            places[name] = (row, rows, len(spans))
+            row += rows
+        spans.append((first, row))
+    return places, spans
+
+
 def force_terms(
     counts, depth, halves, hbm, acc,
-    u, ahead_s, local_s, fixed_s, st, sz, sy, rt, rz, ry, vts, vzs, vys, vtr, vzr, vyr,
-    c01, c10, c02, c20, c12, c21, k01, k10, k02, k20, k12, k21,
-    load_sem, send, recv, ready,
+    u, ahead_s, local_s, fixed_s, outbox, inbox, load_sem, send, recv, ready,
 ):
     g = Lattice(depth)
     last = halves - 1
     me = [lax.axis_index(a) for a in AXES]
-    corner_out = {(0, 1): c01, (1, 0): c10, (0, 2): c02, (2, 0): c20, (1, 2): c12, (2, 1): c21}
-    corner_in = {(0, 1): k01, (1, 0): k10, (0, 2): k02, (2, 0): k20, (1, 2): k12, (2, 1): k21}
-
-    loads = [
-        pltpu.make_async_copy(hbm.at[m, :, 0:2], u.at[m, :, 0:2], load_sem.at[m]) for m in range(4)
-    ]
-    last_rows = pltpu.make_async_copy(hbm.at[:, :, 2], u.at[:, :, 2], load_sem.at[4])
-    for m in (0, 3, 1, 2):
-        loads[m].start()
+    places, spans = mail(depth, halves)
+
+    upper_rows = pltpu.make_async_copy(hbm.at[:, :, 0:2], u.at[:, :, 0:2], load_sem.at[0])
+    last_rows = pltpu.make_async_copy(hbm.at[:, :, 2], u.at[:, :, 2], load_sem.at[1])
+    upper_rows.start()
     last_rows.start()
 
     def peer(kind, sign):
@@ -153,27 +176,51 @@
     def _():
         pl.semaphore_wait(barrier, expected)
 
+    def answer_group(kind, sign):
+        if kind < 3:
+            return 2 if (kind, sign) == (0, -1) else 0
+        return 3 if kind < 5 and sign < 0 else 1
+
     for kind, sign in pairs:
 
         @pl.when(highest(kind, sign))
         def _():
             pl.semaphore_signal(
-                ready.at[2 * kind + (sign > 0)], inc=1,
+                ready.at[answer_group(kind, -sign)], inc=1,
                 device_id=peer(kind, sign), device_id_type=pl.DeviceIdType.MESH,
             )
 
+    def answers(group):
+        count = 0
+        for kind, sign in pairs:
+            if answer_group(kind, sign) == group:
+                count = count + jnp.where(lowest(kind, sign), 1, 0)
+
+        @pl.when(count > 0)
+        def _():
+            pl.semaphore_wait(ready.at[group], count)
+
+    def start(copies):
+        for copy in copies:
+            copy.start()
+
     def early(kind, sign, copies):
-        @pl.when(highest(kind, sign))
-        def _():
-            for copy in copies:
-                copy.start()
+        pl.when(highest(kind, sign))(lambda: start(copies))
 
     def late(kind, sign, copies):
-        @pl.when(lowest(kind, sign))
-        def _():
-            pl.semaphore_wait(ready.at[2 * kind + (sign < 0)], 1)
-            for copy in copies:
-                copy.start()
+        pl.when(lowest(kind, sign))(lambda: start(copies))
+
+    def middle(kind, sign, copies):
+        between = jnp.logical_not(jnp.logical_or(lowest(kind, sign), highest(kind, sign)))
+        pl.when(between)(lambda: start(copies))
+
+    def put(name, r, value):
+        row = places[name][0] + r
+        outbox[row : row + SUB, :] = value
+
+    def got(name, r):
+        row = places[name][0] + r
+        return inbox[row : row + SUB, :]
 
     def load(m, part, i, j, h):
         return u[m, part, i, j, h * SUB : (h + 1) * SUB, :]
@@ -196,61 +243,53 @@
         return total
 
     def pack_t(m):
-        cs, base = comps(m), 12 * others(0).index(m)
+        cs = comps(m)
         for c0 in range(0, 12, g.per):
-            r = (base + c0) // g.per * SUB
-            st[r : r + SUB, :] = merge(
-                [g.rows(load(*cs[c0 + k], 0), depth * k) for k in range(g.per)], g.row, depth
+            put(
+                ("low", 0, m), c0 // g.per * SUB,
+                merge([g.rows(load(*cs[c0 + k], 0), depth * k) for k in range(g.per)], g.row, depth),
             )
 
     def pack_z(m):
-        cs, base = comps(m), 12 * others(1).index(m)
+        cs = comps(m)
         for c0 in range(0, 12, depth):
             for h in range(halves):
-                r = ((base + c0) // depth * halves + h) * SUB
-                sz[r : r + SUB, :] = merge(
-                    [g.rows(load(*cs[c0 + k], h), k) for k in range(depth)], g.zrow, 1
+                put(
+                    ("low", 1, m), (c0 // depth * halves + h) * SUB,
+                    merge([g.rows(load(*cs[c0 + k], h), k) for k in range(depth)], g.zrow, 1),
                 )
 
     def pack_y():
         cs = all_comps(2)
         for c0 in range(0, len(cs), g.ygroups):
             for h in range(halves):
-                r = (c0 // g.ygroups * halves + h) * SUB
-                sy[r : r + SUB, :] = merge(
-                    [
-                        g.lanes(load(*cs[c0 + k], h), NX * k)
-                        for k in range(min(g.ygroups, len(cs) - c0))
-                    ],
-                    g.lane, NX,
+                ks = range(min(g.ygroups, len(cs) - c0))
+                put(
+                    ("low", 2), (c0 // g.ygroups * halves + h) * SUB,
+                    merge([g.lanes(load(*cs[c0 + k], h), NX * k) for k in ks], g.lane, NX),
                 )
 
     def pack_vt(m, v):
-        base = 12 * others(0).index(m)
         for c0 in range(0, 12, g.per):
-            r = (base + c0) // g.per * SUB
-            vts[r : r + SUB, :] = merge(
-                [g.rows(v[c0 + k], depth * (k + 1)) for k in range(g.per)], g.row, depth
+            put(
+                ("high", 0, m), c0 // g.per * SUB,
+                merge([g.rows(v[c0 + k], depth * (k + 1)) for k in range(g.per)], g.row, depth),
             )
 
     def pack_vz(m, h, v):
-        base = 12 * others(1).index(m)
         for c0 in range(0, 12, depth):
-            r = ((base + c0) // depth * halves + h) * SUB
-            vzs[r : r + SUB, :] = merge(
-                [g.rows(v[c0 + k], k + 1 - depth) for k in range(depth)], g.zrow, 1
+            put(
+                ("high", 1, m), (c0 // depth * halves + h) * SUB,
+                merge([g.rows(v[c0 + k], k + 1 - depth) for k in range(depth)], g.zrow, 1),
             )
 
     def pack_vy(m, v):
-        n = vys.shape[0] // 3
+        n = places["high", 2][1] // 3
         for c0 in range(0, 12 * halves, g.ygroups):
-            r = others(2).index(m) * n + c0 // g.ygroups * SUB
-            vys[r : r + SUB, :] = merge(
-                [
-                    g.lanes(v[c0 + k], NX * (k + 1))
-                    for k in range(min(g.ygroups, 12 * halves - c0))
-                ],
-                g.lane, NX,
+            ks = range(min(g.ygroups, 12 * halves - c0))
+            put(
+                ("high", 2), others(2).index(m) * n + c0 // g.ygroups * SUB,
+                merge([g.lanes(v[c0 + k], NX * (k + 1)) for k in ks], g.lane, NX),
             )
 
     def by_groups(d, h, up, shift, index, step):
@@ -270,72 +309,54 @@
         )
 
     def pack_corner(d, m):
-        ref, cs = corner_out[d, m], comps(d)
+        cs = comps(d)
         if (d, m) in ((0, 1), (1, 0)):
             source = SUB - depth if d == 0 else depth - 1
             for c0 in range(0, 12, SUB):
-                ref[c0 : c0 + SUB, :] = merge(
-                    [
-                        g.rows(load(*cs[c0 + k], last if d == 0 else 0), k - source)
-                        for k in range(min(SUB, 12 - c0))
-                    ],
-                    g.row, 1,
-                )
+                ks = range(min(SUB, 12 - c0))
+                values = [g.rows(load(*cs[c0 + k], last if d == 0 else 0), k - source) for k in ks]
+                put((d, m), c0, merge(values, g.row, 1))
         elif (d, m) == (0, 2):
-            ref[...] = by_groups(0, last, 0, lambda k: depth * (k + 1), g.row, depth)
+            put((d, m), 0, by_groups(0, last, 0, lambda k: depth * (k + 1), g.row, depth))
         elif (d, m) == (2, 0):
-            ref[...] = by_groups(2, 0, 1, lambda k: depth * k, g.row, depth)
+            put((d, m), 0, by_groups(2, 0, 1, lambda k: depth * k, g.row, depth))
         else:
             for h in range(halves):
                 up, source = (0, depth - 1) if d == 1 else (1, 0)
-                ref[h * SUB : (h + 1) * SUB, :] = by_groups(
-                    d, h, up, lambda k: k - source, g.zrow, 1
-                )
+                put((d, m), h * SUB, by_groups(d, h, up, lambda k: k - source, g.zrow, 1))
 
     def corner(d, m, h, c):
-        ref = corner_in[d, m]
         k, group = c // g.ygroups, NX * (c % g.ygroups)
         if (d, m) in ((0, 1), (1, 0)):
             target = depth - 1 if d == 0 else SUB - depth
-            r = c // SUB * SUB
-            return g.rows(ref[r : r + SUB, :], target - c % SUB)
+            return g.rows(got((d, m), c // SUB * SUB), target - c % SUB)
         if (d, m) == (0, 2):
-            return g.lanes(g.rows(ref[...], -depth * k), LANES - NX - group)
+            return g.lanes(g.rows(got((d, m), 0), -depth * k), LANES - NX - group)
         if (d, m) == (2, 0):
-            return g.lanes(g.rows(ref[...], SUB - depth - depth * k), -group)
-        value = ref[h * SUB : (h + 1) * SUB, :]
+            return g.lanes(g.rows(got((d, m), 0), SUB - depth - depth * k), -group)
         if d == 1:
-            return g.lanes(g.rows(value, -k), LANES - NX - group)
-        return g.lanes(g.rows(value, depth - 1 - k), -group)
-
-    slots = {}
-
-    def remote(src, dst, kind, sign):
-        slot = len(slots)
-        slots[slot] = pltpu.make_async_remote_copy(
-            src_ref=src, dst_ref=dst, send_sem=send.at[slot], recv_sem=recv.at[slot],
+            return g.lanes(g.rows(got((d, m), h * SUB), -k), LANES - NX - group)
+        return g.lanes(g.rows(got((d, m), h * SUB), depth - 1 - k), -group)
+
+    def remote(first, end, group, kind, sign):
+        return pltpu.make_async_remote_copy(
+            src_ref=outbox.at[first:end], dst_ref=inbox.at[first:end],
+            send_sem=send.at[0], recv_sem=recv.at[group],
             device_id=peer(kind, sign), device_id_type=pl.DeviceIdType.MESH,
         )
-        return slots[slot]
-
-    def chunk(ref, d, m):
-        n = ref.shape[0] // 3
-        k = others(d).index(m)
-        return ref.at[k * n : (k + 1) * n]
-
-    low = {
-        (d, m): remote(chunk(s, d, m), chunk(r, d, m), d, -1)
-        for d, s, r in ((0, st, rt), (1, sz, rz)) for m in others(d)
-    }
-    low[2, None] = remote(sy, ry, 2, -1)
-    high = {
-        (d, m): remote(chunk(s, d, m), chunk(r, d, m), d, 1)
-        for d, s, r in ((0, vts, vtr), (1, vzs, vzr), (2, vys, vyr)) for m in others(d)
-    }
-    corners = {
-        key: remote(corner_out[key], corner_in[key], kind, sign)
-        for key, (kind, sign) in CORNERS.items()
-    }
+
+    def message(name, kind, sign):
+        first, rows, group = places[name]
+        return remote(first, first + rows, group, kind, sign)
+
+    def arrived(name):
+        group = places[name][2]
+        remote(*spans[group], group, 0, 1).wait_recv()
+
+    low = {(d, m): message(("low", d, m), d, -1) for d in (0, 1) for m in others(d)}
+    high = {(d, m): message(("high", d, m), d, 1) for d in (0, 1) for m in others(d)}
+    low_y, high_y = message(("low", 2), 2, -1), message(("high", 2), 2, 1)
+    corners = {key: message(key, kind, sign) for key, (kind, sign) in CORNERS.items()}
 
     def matrix(m, h):
         return [[[load(m, part, i, j, h) for j in range(3)] for i in range(3)] for part in range(2)]
@@ -403,32 +424,40 @@
         save(local_s, PLANES.index((mu, nu)) * halves + h, b)
         return b
 
-    for copy in [loads[m] for m in (0, 3, 1, 2)] + [last_rows]:
-        copy.wait()
+    acc[...] = jnp.zeros_like(acc)
+    upper_rows.wait()
     pack_corner(0, 1)
     pack_corner(0, 2)
+    last_rows.wait()
     for m in (3, 1, 2):
         b = local_product(0, m, last)
         pack_vt(m, transported(b, 0, m, last, False))
-
     above_t, below_t = [high[0, m] for m in (3, 1, 2)], [low[0, m] for m in (3, 1, 2)]
-    above_z, below_z = [high[1, m] for m in (3, 0, 2)], [low[1, m] for m in (3, 2, 0)]
-    above_y, below_y = [high[2, m] for m in (3, 0, 1)], [low[2, None]]
+    below_z = [low[1, m] for m in (3, 0, 2)]
     for d in (1, 2):
         early(*CORNERS[0, d], [corners[0, d]])
     early(0, 1, above_t)
     for m in (3, 1, 2):
         pack_t(m)
     early(0, -1, below_t)
-    for m in (3, 2, 0):
+    for m in (3, 0, 2):
         pack_z(m)
     early(1, -1, below_z)
     pack_y()
-    early(2, -1, below_y)
+    early(2, -1, [low_y])
     for key in ((1, 0), (2, 0), (1, 2), (2, 1)):
         pack_corner(*key)
     for key in ((1, 0), (2, 0), (1, 2), (2, 1)):
         early(*CORNERS[key], [corners[key]])
+    answers(0)
+    late(2, -1, [low_y])
+    late(1, -1, below_z)
+    for key in ((1, 2), (2, 1), (0, 1), (0, 2)):
+        middle(*CORNERS[key], [corners[key]])
+    late(0, 1, above_t)
+    for key in ((1, 0), (2, 0)):
+        between = jnp.logical_and(me[0] > 0, jnp.logical_not(highest(*CORNERS[key])))
+        pl.when(between)(corners[key].start)
 
     lifted = {}
 
@@ -454,30 +483,18 @@
                 pack_vy(m, [x for h in range(halves) for x in lifted[d, m, h]])
 
     lift(1, 3)
+    high[1, 3].start()
     lift(0, 1)
+    high[1, 0].start()
     lift(1, 2)
-    early(1, 1, above_z)
-    late(1, -1, below_z)
-    late(0, 1, above_t)
-    late(2, -1, below_y)
-    late(1, 1, above_z)
+    high[1, 2].start()
     lift(2, 3)
     lift(0, 2)
-    early(2, 1, above_y)
-    late(2, 1, above_y)
+    high_y.start()
     lift(0, 3)
+    answers(1)
     for key in ((0, 1), (0, 2), (1, 2), (2, 1)):
         late(*CORNERS[key], [corners[key]])
-
-        @pl.when(jnp.logical_not(jnp.logical_or(lowest(*CORNERS[key]), highest(*CORNERS[key]))))
-        def _():
-            corners[key].start()
-
-    for key in ((1, 0), (2, 0)):
-
-        @pl.when(jnp.logical_and(me[0] > 0, jnp.logical_not(highest(*CORNERS[key]))))
-        def _():
-            corners[key].start()
 
     def ahead(m, d, h):
         if complete(d, h):
@@ -487,15 +504,15 @@
         def get(part, i, j):
             v = ahead_s[ahead_slot[m, d, h], part, i, j]
             c = index[(m, part, i, j)]
+            k = c % 12
             if d == 0:
-                r = c // g.per * SUB
-                edge = g.rows(rt[r : r + SUB, :], SUB - depth - depth * (c % g.per))
+                edge = g.rows(got(("low", 0, m), k // g.per * SUB), SUB - depth - depth * (k % g.per))
             elif d == 1:
-                r = (c // depth * halves + h) * SUB
-                edge = g.rows(rz[r : r + SUB, :], depth - 1 - c % depth)
+                edge = g.rows(got(("low", 1, m), (k // depth * halves + h) * SUB), depth - 1 - k % depth)
             else:
-                r = (c // g.ygroups * halves + h) * SUB
-                edge = g.lanes(ry[r : r + SUB, :], LANES - NX - NX * (c % g.ygroups))
+                edge = g.lanes(
+                    got(("low", 2), (c // g.ygroups * halves + h) * SUB), LANES - NX - NX * (c % g.ygroups)
+                )
             return jnp.where(far_edge(d), edge, v)
 
         return complete_rows(get)
@@ -506,15 +523,9 @@
         third_r, third_i = third_row(real, imag)
         return [real + [third_r], imag + [third_i]]
 
-    seen = set()
-
     def add(m, c, h, value):
         r = ((m * 8 + c) * halves + h) * SUB
-        if (m, c, h) in seen:
-            acc[r : r + SUB, :] += value
-        else:
-            seen.add((m, c, h))
-            acc[r : r + SUB, :] = value
+        acc[r : r + SUB, :] += value
 
     def shifted(q, d):
         if d == 3:
@@ -555,16 +566,13 @@
     def lower(d, m, h):
         def get(part, i, j):
             c = part * 6 + i * 3 + j
-            base = 12 * others(d).index(m) + c
             if d == 0:
-                r = base // g.per * SUB
-                return g.rows(vtr[r : r + SUB, :], -depth * (base % g.per))
+                return g.rows(got(("high", 0, m), c // g.per * SUB), -depth * (c % g.per))
             if d == 1:
-                r = (base // depth * halves + h) * SUB
-                return g.rows(vzr[r : r + SUB, :], -(base % depth))
-            n, k = vyr.shape[0] // 3, h * 12 + c
+                return g.rows(got(("high", 1, m), (c // depth * halves + h) * SUB), -(c % depth))
+            n, k = places["high", 2][1] // 3, h * 12 + c
             r = others(2).index(m) * n + k // g.ygroups * SUB
-            return g.lanes(vyr[r : r + SUB, :], -NX * (k % g.ygroups))
+            return g.lanes(got(("high", 2), r), -NX * (k % g.ygroups))
 
         if (d, m, h) in fixed_slot:
             left = saved(fixed_s, fixed_slot[d, m, h])
@@ -575,54 +583,81 @@
         for c in range(8):
             add(m, c, h, jnp.where(near, q[c], 0.0))
 
+    def y_part():
+        arrived(("low", 2))
+        for h in range(halves):
+            plane(2, 3, h)
+        for h in range(last):
+            plane(0, 2, h)
+
+    def z_part():
+        arrived(("low", 1, 3))
+        for h in range(halves):
+            plane(1, 3, h)
+        arrived(("low", 1, 0))
+        for h in range(last):
+            plane(0, 1, h)
+
+    def around_part():
+        answers(2)
+        late(0, -1, below_t)
+
     for h in range(last):
         plane(0, 3, h)
-    low[2, None].wait_recv()
-    for h in range(halves):
-        plane(2, 3, h)
-    for h in range(last):
-        plane(0, 2, h)
-    late(0, -1, below_t)
+    even = lax.rem(me[2], 2) == 0
+
+    @pl.when(even)
+    def _():
+        y_part()
+        around_part()
+        z_part()
+
+    @pl.when(jnp.logical_not(even))
+    def _():
+        around_part()
+        z_part()
+        y_part()
+
+    answers(3)
     for key in ((1, 0), (2, 0)):
-        late(*CORNERS[key], [corners[key]])
-
-        @pl.when(jnp.logical_and(me[0] == 0, jnp.logical_not(lowest(*CORNERS[key]))))
-        def _():
-            corners[key].start()
-
-    low[1, 3].wait_recv()
-    for h in range(halves):
-        plane(1, 3, h)
-    low[1, 2].wait_recv()
+        first = jnp.logical_and(me[0] == 0, jnp.logical_not(highest(*CORNERS[key])))
+        pl.when(first)(corners[key].start)
+
+    arrived(("low", 1, 2))
     for h in range(halves):
         plane(1, 2, h)
-    low[1, 0].wait_recv()
-    for h in range(last):
-        plane(0, 1, h)
-
-    for d, m in ((2, 3), (2, 1), (2, 0), (1, 3), (1, 2), (1, 0)):
-        if (d, m) in ((2, 1), (1, 2)):
-            corners[d, m].wait_recv()
-            for h in range(halves):
-                fix(d, m, h)
-        high[d, m].wait_recv()
+    arrived(("high", 2))
+    for h in range(halves):
+        fix(2, 1, h)
+    for m in (3, 1, 0):
         for h in range(halves if m else last):
-            lower(d, m, h)
-    for m in (3, 1, 2):
-        low[0, m].wait_recv()
-        plane(0, m, last)
+            lower(2, m, h)
+    arrived(("low", 0, 3))
+    plane(0, 3, last)
+    arrived(("low", 0, 1))
+    plane(0, 1, last)
+    plane(0, 2, last)
+    arrived(("high", 1, 3))
+    for m in (3, 0):
+        for h in range(halves if m else last):
+            lower(1, m, h)
+    arrived(("high", 1, 2))
+    for h in range(halves):
+        fix(1, 2, h)
+        lower(1, 2, h)
+    arrived((1, 0))
     for d in (1, 2):
-        corners[d, 0].wait_recv()
         fix(d, 0, last)
         lower(d, 0, last)
+    arrived(("high", 0, 3))
     for m in (1, 2):
-        corners[0, m].wait_recv()
         fix(0, m, 0)
-    for m in (3, 1, 2):
-        high[0, m].wait_recv()
-        lower(0, m, 0)
-    for copy in slots.values():
-        copy.wait_send()
+    lower(0, 3, 0)
+    arrived(("high", 0, 1))
+    lower(0, 1, 0)
+    arrived(("high", 0, 2))
+    lower(0, 2, 0)
+    remote(0, spans[-1][1], 0, 0, 1).wait_send()
 
 
 def expand(halves, acc, hbm, out, sems):
@@ -656,13 +691,9 @@
     sites = time_len * depth
     assert flat == LANES and SUB % depth == 0 and sites % SUB == 0 and 2 <= depth <= SUB // 2
     halves = sites // SUB
-    per, yg = SUB // depth, LANES // NX
-    up = lambda a, b: -(-a // b) * SUB
+    spans = mail(depth, halves)[1]
     vmem = lambda *s: pltpu.VMEM(s + (LANES,), jnp.float32)
     shape = links.shape[:4] + (sites, flat)
-    rt, rz, ry = up(36, per), up(36, depth) * halves, up(36, yg) * halves
-    vy = 3 * up(12 * halves, yg)
-    corner = [vmem(r) for r in (2 * SUB, 2 * SUB, SUB, SUB, SUB * halves, SUB * halves)]
     terms = pl.pallas_call(
         functools.partial(force_terms, counts, depth, halves),
         out_shape=pltpu.VMEM((32 * sites, flat), jnp.float32),
@@ -673,14 +704,12 @@
             vmem(12 * halves, 2, 3, 3, SUB),
             vmem(6 * halves, 2, 3, 3, SUB),
             vmem(4 + 2 * halves, 2, 3, 3, SUB),
-        ]
-        + [vmem(r) for r in (rt, rz, ry) * 2 + (rt, rz, vy) * 2]
-        + corner * 2
-        + [
-            pltpu.SemaphoreType.DMA((5,)),
-            pltpu.SemaphoreType.DMA((22,)),
-            pltpu.SemaphoreType.DMA((22,)),
-            pltpu.SemaphoreType.REGULAR((12,)),
+            vmem(spans[-1][1]),
+            vmem(spans[-1][1]),
+            pltpu.SemaphoreType.DMA((2,)),
+            pltpu.SemaphoreType.DMA((1,)),
+            pltpu.SemaphoreType.DMA((len(spans),)),
+            pltpu.SemaphoreType.REGULAR((4,)),
         ],
         compiler_params=pltpu.CompilerParams(collective_id=0, has_side_effects=True),
         name="force_terms",

time: 11.7 us -> 10.8 us (0.923)
  the two profiles are of different devices: /device:TPU:1 before, /device:TPU:7 now
where the time goes in v3:
time: 10.8 us; the launch traced here: 10.6 us
  Pallas kernels  10.6 us (98%)
    pallas_call x1, Pallas kernels, per_device(): pl.pallas_call(functools.partial(force_terms, counts, depth, halves), out...  9.76 us
    pallas_call x1, Pallas kernels, per_device(): pl.pallas_call(functools.partial(expand, halves), out_shape=jax.ShapeDtyp...  0.86 us

profile of v3, /device:TPU:7, one launch (start us, length us, event | category | flops | bytes accessed | tf_op | source)
XLA Modules:
  0.0 10.6 jit_solution(12942776996699554444)
XLA Ops:
  0.0 9.8 %force_terms.1.acc = f32[512,128]{1,0:T(8,128)S(1)} custom-call(f32[4,2,3,3,16,128]{5,4,3,2,1,0:T(8,128)} %bitcast.2), custom_call_target="tpu_custom_call" | custom-call | tf_op jit(solution)/shard_map/force_terms/pallas_call | solution.py:697
  9.8 0.9 %expand.1 = f32[4,2,3,3,16,128]{5,4,3,2,1,0:T(8,128)} custom-call(f32[512,128]{1,0:T(8,128)S(1)} %force_terms.1.acc), custom_call_target="tpu_custom_call" | custom-call | tf_op jit(solution)/shard_map/expand/pallas_call | solution.py:717

commit v4 on v3

--- a/solution.py
+++ b/solution.py
@@ -99,24 +99,58 @@
 FIXED = [(0, 1, 0), (0, 2, 0), (1, 0, -1), (1, 2, None), (2, 0, -1), (2, 1, None)]
 
 
+def by_largest(real, imag):
+    size = [jnp.maximum(jnp.abs(r), jnp.abs(i)) for r, i in zip(real, imag)]
+    first = jnp.logical_and(size[0] >= size[1], size[0] >= size[2])
+    second = size[1] >= size[2]
+    return lambda a, b, c: jnp.where(first, a, jnp.where(second, b, c))
+
+
+def shortened(v):
+    pick = by_largest(v[0:3], v[6:9])
+    keep = v[0:3] + v[6:9]
+    for turn in (1, 2):
+        for row in (v[3:6], v[9:12]):
+            keep.append(pick(*(row[(k + turn) % 3] for k in range(3))))
+    return keep
+
+
+def restored(v):
+    real, imag = v[0:3], v[3:6]
+    pick = by_largest(real, imag)
+    (xr, xi), (yr, yi), (zr, zi) = (
+        [pick(*(part[(k + turn) % 3] for k in range(3))) for part in (real, imag)] for turn in range(3)
+    )
+    pr, pi, qr, qi = v[6:10]
+    sr = pr * yr + pi * yi + qr * zr + qi * zi
+    si = pi * yr - pr * yi + qi * zr - qr * zi
+    scale = -1.0 / (xr * xr + xi * xi)
+    br, bi = (sr * xr - si * xi) * scale, (sr * xi + si * xr) * scale
+    second_r = [pick(br, qr, pr), pick(pr, br, qr), pick(qr, pr, br)]
+    second_i = [pick(bi, qi, pi), pick(pi, bi, qi), pick(qi, pi, bi)]
+    third_r, third_i = third_row([real, second_r], [imag, second_i])
+    return [[real, second_r, third_r], [imag, second_i, third_i]]
+
+
 def mail(depth, halves):
     up = lambda a, b: -(-a // b) * SUB
     per, yg = SUB // depth, LANES // NX
     t, z, y = up(12, per), up(12, depth) * halves, up(36, yg) * halves
+    short = up(10, per)
     groups = (
         ((("low", 2), y),),
         ((("low", 1, 3), z),),
         ((("low", 1, 0), z),),
         ((("low", 1, 2), z),),
-        ((("high", 2), 3 * up(12 * halves, yg)), ((2, 1), SUB * halves)),
-        ((("high", 1, 3), z), (("high", 1, 0), z)),
-        ((("high", 1, 2), z), ((1, 2), SUB * halves)),
+        ((("high", 2), 3 * up(12 * halves, yg)),),
+        ((("high", 1, 3), z), (("high", 1, 0), z), (("high", 1, 2), z)),
         ((("low", 0, 3), t),),
         ((("low", 0, 1), t), (("low", 0, 2), t)),
+        (((2, 1), SUB * halves), ((1, 2), SUB * halves)),
         (((1, 0), 2 * SUB), ((2, 0), SUB)),
-        ((("high", 0, 3), t), ((0, 1), 2 * SUB), ((0, 2), SUB)),
-        ((("high", 0, 1), t),),
-        ((("high", 0, 2), t),),
+        ((("high", 0, 3), short), (("high", 0, 2), short)),
+        (((0, 1), 2 * SUB), ((0, 2), SUB)),
+        ((("high", 0, 1), short),),
     )
     places, spans, row = {}, [], 0
     for group in groups:
@@ -137,10 +171,15 @@
     me = [lax.axis_index(a) for a in AXES]
     places, spans = mail(depth, halves)
 
-    upper_rows = pltpu.make_async_copy(hbm.at[:, :, 0:2], u.at[:, :, 0:2], load_sem.at[0])
-    last_rows = pltpu.make_async_copy(hbm.at[:, :, 2], u.at[:, :, 2], load_sem.at[1])
-    upper_rows.start()
-    last_rows.start()
+    cut = last * SUB
+    load_last = pltpu.make_async_copy(
+        hbm.at[:, :, :, :, cut:], u.at[:, :, :, :, cut:], load_sem.at[0]
+    )
+    load_rest = pltpu.make_async_copy(
+        hbm.at[:, :, :, :, :cut], u.at[:, :, :, :, :cut], load_sem.at[1]
+    )
+    load_last.start()
+    load_rest.start()
 
     def peer(kind, sign):
         where = list(me)
@@ -270,10 +309,12 @@
                 )
 
     def pack_vt(m, v):
-        for c0 in range(0, 12, g.per):
+        v = shortened(v)
+        for c0 in range(0, 10, g.per):
+            ks = range(min(g.per, 10 - c0))
             put(
                 ("high", 0, m), c0 // g.per * SUB,
-                merge([g.rows(v[c0 + k], depth * (k + 1)) for k in range(g.per)], g.row, depth),
+                merge([g.rows(v[c0 + k], depth * (k + 1)) for k in ks], g.row, depth),
             )
 
     def pack_vz(m, h, v):
@@ -424,40 +465,36 @@
         save(local_s, PLANES.index((mu, nu)) * halves + h, b)
         return b
 
+    below_t, below_z = [low[0, m] for m in (3, 1, 2)], [low[1, m] for m in (3, 0, 2)]
+    above_t = [high[0, m] for m in (3, 2, 1)]
+    at_end = me[0] == counts[0] - 1
+
+    def faces():
+        load_rest.wait()
+        for m in (3, 1, 2):
+            pack_t(m)
+        early(0, -1, below_t)
+        for m in (3, 0, 2):
+            pack_z(m)
+        early(1, -1, below_z)
+
     acc[...] = jnp.zeros_like(acc)
-    upper_rows.wait()
-    pack_corner(0, 1)
-    pack_corner(0, 2)
-    last_rows.wait()
-    for m in (3, 1, 2):
+    load_last.wait()
+    for d in (1, 2):
+        pack_corner(0, d)
+        early(*CORNERS[0, d], [corners[0, d]])
+    pl.when(jnp.logical_not(at_end))(faces)
+    for m in (3, 2, 1):
         b = local_product(0, m, last)
         pack_vt(m, transported(b, 0, m, last, False))
-    above_t, below_t = [high[0, m] for m in (3, 1, 2)], [low[0, m] for m in (3, 1, 2)]
-    below_z = [low[1, m] for m in (3, 0, 2)]
-    for d in (1, 2):
-        early(*CORNERS[0, d], [corners[0, d]])
-    early(0, 1, above_t)
-    for m in (3, 1, 2):
-        pack_t(m)
-    early(0, -1, below_t)
-    for m in (3, 0, 2):
-        pack_z(m)
-    early(1, -1, below_z)
+        early(0, 1, [high[0, m]])
+    pl.when(at_end)(faces)
     pack_y()
     early(2, -1, [low_y])
     for key in ((1, 0), (2, 0), (1, 2), (2, 1)):
         pack_corner(*key)
     for key in ((1, 0), (2, 0), (1, 2), (2, 1)):
         early(*CORNERS[key], [corners[key]])
-    answers(0)
-    late(2, -1, [low_y])
-    late(1, -1, below_z)
-    for key in ((1, 2), (2, 1), (0, 1), (0, 2)):
-        middle(*CORNERS[key], [corners[key]])
-    late(0, 1, above_t)
-    for key in ((1, 0), (2, 0)):
-        between = jnp.logical_and(me[0] > 0, jnp.logical_not(highest(*CORNERS[key])))
-        pl.when(between)(corners[key].start)
 
     lifted = {}
 
@@ -482,12 +519,24 @@
             elif d == 2:
                 pack_vy(m, [x for h in range(halves) for x in lifted[d, m, h]])
 
+    def greeted():
+        answers(0)
+        late(2, -1, [low_y])
+        for key in ((0, 1), (0, 2), (1, 2), (2, 1)):
+            middle(*CORNERS[key], [corners[key]])
+        late(1, -1, below_z)
+        late(0, 1, above_t)
+        for key in ((1, 0), (2, 0)):
+            between = jnp.logical_and(me[0] > 0, jnp.logical_not(highest(*CORNERS[key])))
+            pl.when(between)(corners[key].start)
+
+    pl.when(at_end)(greeted)
     lift(1, 3)
-    high[1, 3].start()
     lift(0, 1)
-    high[1, 0].start()
     lift(1, 2)
-    high[1, 2].start()
+    pl.when(jnp.logical_not(at_end))(greeted)
+    for m in (3, 0, 2):
+        high[1, m].start()
     lift(2, 3)
     lift(0, 2)
     high_y.start()
@@ -566,8 +615,6 @@
     def lower(d, m, h):
         def get(part, i, j):
             c = part * 6 + i * 3 + j
-            if d == 0:
-                return g.rows(got(("high", 0, m), c // g.per * SUB), -depth * (c % g.per))
             if d == 1:
                 return g.rows(got(("high", 1, m), (c // depth * halves + h) * SUB), -(c % depth))
             n, k = places["high", 2][1] // 3, h * 12 + c
@@ -578,7 +625,13 @@
             left = saved(fixed_s, fixed_slot[d, m, h])
         else:
             left = matrix(m, h)
-        q = projected(left, complete_rows(get), right_h=True)
+        if d == 0:
+            lifts = restored(
+                [g.rows(got(("high", 0, m), c // g.per * SUB), -depth * (c % g.per)) for c in range(10)]
+            )
+        else:
+            lifts = complete_rows(get)
+        q = projected(left, lifts, right_h=True)
         near = (g.row < depth, g.zrow == 0, g.lane < NX)[d]
         for c in range(8):
             add(m, c, h, jnp.where(near, q[c], 0.0))
@@ -594,13 +647,15 @@
         arrived(("low", 1, 3))
         for h in range(halves):
             plane(1, 3, h)
+
+    def around_part():
+        answers(2)
+        late(0, -1, below_t)
+
+    def rest_part():
         arrived(("low", 1, 0))
         for h in range(last):
             plane(0, 1, h)
-
-    def around_part():
-        answers(2)
-        late(0, -1, below_t)
 
     for h in range(last):
         plane(0, 3, h)
@@ -611,11 +666,13 @@
         y_part()
         around_part()
         z_part()
+        rest_part()
 
     @pl.when(jnp.logical_not(even))
     def _():
+        z_part()
         around_part()
-        z_part()
+        rest_part()
         y_part()
 
     answers(3)
@@ -627,9 +684,7 @@
     for h in range(halves):
         plane(1, 2, h)
     arrived(("high", 2))
-    for h in range(halves):
-        fix(2, 1, h)
-    for m in (3, 1, 0):
+    for m in (3, 0):
         for h in range(halves if m else last):
             lower(2, m, h)
     arrived(("low", 0, 3))
@@ -637,26 +692,27 @@
     arrived(("low", 0, 1))
     plane(0, 1, last)
     plane(0, 2, last)
+    arrived((2, 1))
+    for h in range(halves):
+        fix(2, 1, h)
+        lower(2, 1, h)
+        fix(1, 2, h)
+    arrived((1, 0))
+    fix(2, 0, last)
+    lower(2, 0, last)
+    fix(1, 0, last)
     arrived(("high", 1, 3))
-    for m in (3, 0):
-        for h in range(halves if m else last):
+    for m in (3, 0, 2):
+        for h in range(halves):
             lower(1, m, h)
-    arrived(("high", 1, 2))
-    for h in range(halves):
-        fix(1, 2, h)
-        lower(1, 2, h)
-    arrived((1, 0))
-    for d in (1, 2):
-        fix(d, 0, last)
-        lower(d, 0, last)
     arrived(("high", 0, 3))
-    for m in (1, 2):
-        fix(0, m, 0)
     lower(0, 3, 0)
+    arrived((0, 1))
+    fix(0, 2, 0)
+    fix(0, 1, 0)
+    lower(0, 2, 0)
     arrived(("high", 0, 1))
     lower(0, 1, 0)
-    arrived(("high", 0, 2))
-    lower(0, 2, 0)
     remote(0, spans[-1][1], 0, 0, 1).wait_send()
 
 

time: 10.8 us -> 10.3 us (0.954)
  the two profiles are of different devices: /device:TPU:7 before, /device:TPU:0 now
where the time goes in v4:
time: 10.3 us; the launch traced here: 10.2 us
  Pallas kernels  10.2 us (99%)
    pallas_call x1, Pallas kernels, per_device(): pl.pallas_call(functools.partial(force_terms, counts, depth, halves), out...  9.32 us
    pallas_call x1, Pallas kernels, per_device(): pl.pallas_call(functools.partial(expand, halves), out_shape=jax.ShapeDtyp...  0.86 us

profile of v4, /device:TPU:0, one launch (start us, length us, event | category | flops | bytes accessed | tf_op | source)
XLA Modules:
  0.0 10.2 jit_solution(3848284455952690156)
XLA Ops:
  0.0 9.3 %force_terms.1.acc = f32[512,128]{1,0:T(8,128)S(1)} custom-call(f32[4,2,3,3,16,128]{5,4,3,2,1,0:T(8,128)} %bitcast.2), custom_call_target="tpu_custom_call" | custom-call | tf_op jit(solution)/shard_map/force_terms/pallas_call | solution.py:753
  9.3 0.9 %expand.1 = f32[4,2,3,3,16,128]{5,4,3,2,1,0:T(8,128)} custom-call(f32[512,128]{1,0:T(8,128)S(1)} %force_terms.1.acc), custom_call_target="tpu_custom_call" | custom-call | tf_op jit(solution)/shard_map/expand/pallas_call | solution.py:773

commit v5 on v4

--- a/solution.py
+++ b/solution.py
@@ -146,11 +146,10 @@
         ((("high", 1, 3), z), (("high", 1, 0), z), (("high", 1, 2), z)),
         ((("low", 0, 3), t),),
         ((("low", 0, 1), t), (("low", 0, 2), t)),
-        (((2, 1), SUB * halves), ((1, 2), SUB * halves)),
-        (((1, 0), 2 * SUB), ((2, 0), SUB)),
-        ((("high", 0, 3), short), (("high", 0, 2), short)),
+        (((2, 1), SUB * halves), ((1, 2), SUB * halves), ((1, 0), 2 * SUB), ((2, 0), SUB)),
+        ((("high", 0, 3), short),),
         (((0, 1), 2 * SUB), ((0, 2), SUB)),
-        ((("high", 0, 1), short),),
+        ((("high", 0, "pair"), 10 * SUB),),
     )
     places, spans, row = {}, [], 0
     for group in groups:
@@ -172,14 +171,19 @@
     places, spans = mail(depth, halves)
 
     cut = last * SUB
-    load_last = pltpu.make_async_copy(
-        hbm.at[:, :, :, :, cut:], u.at[:, :, :, :, cut:], load_sem.at[0]
-    )
-    load_rest = pltpu.make_async_copy(
-        hbm.at[:, :, :, :, :cut], u.at[:, :, :, :, :cut], load_sem.at[1]
-    )
-    load_last.start()
-    load_rest.start()
+    cut = last * SUB
+
+    def loads(m, p, from_last):
+        rows = slice(cut, None) if from_last else slice(0, cut)
+        return pltpu.make_async_copy(
+            hbm.at[m, p, :, :, rows], u.at[m, p, :, :, rows], load_sem.at[1 - from_last]
+        )
+
+    for from_last in (1, 0):
+        for m in (0, 3, 2, 1):
+            for p in range(2):
+                loads(m, p, from_last).start()
+    load_last, load_rest = loads(slice(None), slice(None), 1), loads(slice(None), slice(None), 0)
 
     def peer(kind, sign):
         where = list(me)
@@ -189,7 +193,8 @@
         return (by["gx"], by["gz"], by["ta"])
 
     def above(axis, sign):
-        return me[axis] < counts[axis] - 1 if sign > 0 else me[axis] == 0
+        rank = lambda i: i + 1 - 2 * lax.rem(i, 2) if False else i
+        return rank(lax.rem(me[axis] + counts[axis] + sign, counts[axis])) > rank(me[axis])
 
     def lowest(kind, sign):
         tests = [above(i, sign * step) for i, step in KINDS[kind].items()]
@@ -308,14 +313,18 @@
                     merge([g.lanes(load(*cs[c0 + k], h), NX * k) for k in ks], g.lane, NX),
                 )
 
-    def pack_vt(m, v):
+    def pack_vt(v):
         v = shortened(v)
         for c0 in range(0, 10, g.per):
             ks = range(min(g.per, 10 - c0))
             put(
-                ("high", 0, m), c0 // g.per * SUB,
+                ("high", 0, 3), c0 // g.per * SUB,
                 merge([g.rows(v[c0 + k], depth * (k + 1)) for k in ks], g.row, depth),
             )
+
+    def pack_pair(one, two):
+        for c, (v, w) in enumerate(zip(shortened(one), shortened(two))):
+            put(("high", 0, "pair"), c * SUB, jnp.where(g.row >= depth, g.rows(w, 2 * depth), g.rows(v, depth)))
 
     def pack_vz(m, h, v):
         for c0 in range(0, 12, depth):
@@ -395,7 +404,7 @@
         remote(*spans[group], group, 0, 1).wait_recv()
 
     low = {(d, m): message(("low", d, m), d, -1) for d in (0, 1) for m in others(d)}
-    high = {(d, m): message(("high", d, m), d, 1) for d in (0, 1) for m in others(d)}
+    high = {(d, m): message(("high", d, m), d, 1) for d, m in ((0, 3), (0, "pair"), (1, 0), (1, 2), (1, 3))}
     low_y, high_y = message(("low", 2), 2, -1), message(("high", 2), 2, 1)
     corners = {key: message(key, kind, sign) for key, (kind, sign) in CORNERS.items()}
 
@@ -466,17 +475,20 @@
         return b
 
     below_t, below_z = [low[0, m] for m in (3, 1, 2)], [low[1, m] for m in (3, 0, 2)]
-    above_t = [high[0, m] for m in (3, 2, 1)]
+    above_t = [high[0, 3], high[0, "pair"]]
+    even = lax.rem(me[2], 2) == 0
     at_end = me[0] == counts[0] - 1
 
     def faces():
         load_rest.wait()
         for m in (3, 1, 2):
             pack_t(m)
-        early(0, -1, below_t)
+        pl.when(jnp.logical_not(at_end))(lambda: early(0, -1, below_t))
         for m in (3, 0, 2):
             pack_z(m)
         early(1, -1, below_z)
+        pack_y()
+        early(2, -1, [low_y])
 
     acc[...] = jnp.zeros_like(acc)
     load_last.wait()
@@ -484,13 +496,11 @@
         pack_corner(0, d)
         early(*CORNERS[0, d], [corners[0, d]])
     pl.when(jnp.logical_not(at_end))(faces)
-    for m in (3, 2, 1):
-        b = local_product(0, m, last)
-        pack_vt(m, transported(b, 0, m, last, False))
-        early(0, 1, [high[0, m]])
+    pack_vt(transported(local_product(0, 3, last), 0, 3, last, False))
+    early(0, 1, [high[0, 3]])
+    pack_pair(*(transported(local_product(0, m, last), 0, m, last, False) for m in (1, 2)))
+    early(0, 1, [high[0, "pair"]])
     pl.when(at_end)(faces)
-    pack_y()
-    early(2, -1, [low_y])
     for key in ((1, 0), (2, 0), (1, 2), (2, 1)):
         pack_corner(*key)
     for key in ((1, 0), (2, 0), (1, 2), (2, 1)):
@@ -524,6 +534,7 @@
         late(2, -1, [low_y])
         for key in ((0, 1), (0, 2), (1, 2), (2, 1)):
             middle(*CORNERS[key], [corners[key]])
+        pl.when(at_end)(lambda: start(below_t))
         late(1, -1, below_z)
         late(0, 1, above_t)
         for key in ((1, 0), (2, 0)):
@@ -626,9 +637,8 @@
         else:
             left = matrix(m, h)
         if d == 0:
-            lifts = restored(
-                [g.rows(got(("high", 0, m), c // g.per * SUB), -depth * (c % g.per)) for c in range(10)]
-            )
+            values = [got(("high", 0, 3), c // g.per * SUB) for c in range(10)]
+            lifts = restored([g.rows(v, -depth * (c % g.per)) for c, v in enumerate(values)])
         else:
             lifts = complete_rows(get)
         q = projected(left, lifts, right_h=True)
@@ -636,6 +646,37 @@
         for c in range(8):
             add(m, c, h, jnp.where(near, q[c], 0.0))
 
+    pair_slot = 2 + 2 * halves
+
+    def pair_left():
+        one, two = matrix(1, 0), matrix(2, 0)
+        both = lambda p, i, j: jnp.where(g.row >= depth, g.rows(two[p][i][j], depth), one[p][i][j])
+        save(fixed_s, pair_slot, [[[both(p, i, j) for j in range(3)] for i in range(3)] for p in range(2)])
+
+    def pair_fix():
+        def beyond(part, i, j):
+            c = part * 6 + i * 3 + j
+            k = c // g.ygroups
+            value = g.lanes(
+                g.rows(got((0, 2), 0), depth - depth * k), LANES - NX - NX * (c % g.ygroups)
+            )
+            return jnp.where(g.row >= depth, value, corner(0, 1, 0, c))
+
+        own = saved(fixed_s, pair_slot)
+        moved = product(own, complete_rows(beyond), right_h=True)
+        edge = jnp.where(g.row >= depth, g.lane - (LANES - NX - 1), g.row - (depth - 2)) > 0
+        save(
+            fixed_s, pair_slot,
+            [[[jnp.where(edge, moved[p][i][j], own[p][i][j]) for j in range(3)] for i in range(3)] for p in range(2)],
+        )
+
+    def pair_lower():
+        lifts = restored([got(("high", 0, "pair"), c * SUB) for c in range(10)])
+        q = projected(saved(fixed_s, pair_slot), lifts, right_h=True)
+        for c in range(8):
+            add(1, c, 0, jnp.where(g.row < depth, q[c], 0.0))
+            add(2, c, 0, jnp.where(g.row < depth, g.rows(q[c], -depth), 0.0))
+
     def y_part():
         arrived(("low", 2))
         for h in range(halves):
@@ -650,6 +691,9 @@
 
     def around_part():
         answers(2)
+        for key in ((1, 0), (2, 0)):
+            between = jnp.logical_not(jnp.logical_or(lowest(*CORNERS[key]), highest(*CORNERS[key])))
+            pl.when(jnp.logical_and(me[0] == 0, between))(corners[key].start)
         late(0, -1, below_t)
 
     def rest_part():
@@ -657,38 +701,49 @@
         for h in range(last):
             plane(0, 1, h)
 
+    def high_y_part():
+        arrived(("high", 2))
+        for m in (3, 0):
+            for h in range(halves if m else last):
+                lower(2, m, h)
+
+    def t_part():
+        arrived(("low", 0, 3))
+        plane(0, 3, last)
+
+    def corner_part():
+        answers(3)
+        for key in ((1, 0), (2, 0)):
+            pl.when(me[0] == 0)(functools.partial(late, *CORNERS[key], [corners[key]]))
+
     for h in range(last):
         plane(0, 3, h)
-    even = lax.rem(me[2], 2) == 0
-
     @pl.when(even)
     def _():
         y_part()
         around_part()
         z_part()
         rest_part()
+        corner_part()
+        t_part()
+        arrived(("low", 1, 2))
+        for h in range(halves):
+            plane(1, 2, h)
+        high_y_part()
 
     @pl.when(jnp.logical_not(even))
     def _():
         z_part()
         around_part()
         rest_part()
+        high_y_part()
+        corner_part()
+        t_part()
         y_part()
-
-    answers(3)
-    for key in ((1, 0), (2, 0)):
-        first = jnp.logical_and(me[0] == 0, jnp.logical_not(highest(*CORNERS[key])))
-        pl.when(first)(corners[key].start)
-
-    arrived(("low", 1, 2))
-    for h in range(halves):
-        plane(1, 2, h)
-    arrived(("high", 2))
-    for m in (3, 0):
-        for h in range(halves if m else last):
-            lower(2, m, h)
-    arrived(("low", 0, 3))
-    plane(0, 3, last)
+        arrived(("low", 1, 2))
+        for h in range(halves):
+            plane(1, 2, h)
+
     arrived(("low", 0, 1))
     plane(0, 1, last)
     plane(0, 2, last)
@@ -697,10 +752,10 @@
         fix(2, 1, h)
         lower(2, 1, h)
         fix(1, 2, h)
-    arrived((1, 0))
     fix(2, 0, last)
     lower(2, 0, last)
     fix(1, 0, last)
+    pair_left()
     arrived(("high", 1, 3))
     for m in (3, 0, 2):
         for h in range(halves):
@@ -708,11 +763,9 @@
     arrived(("high", 0, 3))
     lower(0, 3, 0)
     arrived((0, 1))
-    fix(0, 2, 0)
-    fix(0, 1, 0)
-    lower(0, 2, 0)
-    arrived(("high", 0, 1))
-    lower(0, 1, 0)
+    pair_fix()
+    arrived(("high", 0, "pair"))
+    pair_lower()
     remote(0, spans[-1][1], 0, 0, 1).wait_send()
 
 
@@ -759,7 +812,7 @@
             vmem(*shape[:-1]),
             vmem(12 * halves, 2, 3, 3, SUB),
             vmem(6 * halves, 2, 3, 3, SUB),
-            vmem(4 + 2 * halves, 2, 3, 3, SUB),
+            vmem(3 + 2 * halves, 2, 3, 3, SUB),
             vmem(spans[-1][1]),
             vmem(spans[-1][1]),
             pltpu.SemaphoreType.DMA((2,)),

time: 10.3 us -> 10.1 us (0.981)
  Pallas kernels: 10.2 us -> 9.94 us
    pallas_call x1, Pallas kernels: 9.32 us -> 9.08 us  [per_device(): pl.pallas_call(functools.partial(force_terms, counts, depth, halves), out...]
where the time goes in v5:
time: 10.1 us; the launch traced here: 9.95 us
  Pallas kernels  9.94 us (98%)
    pallas_call x1, Pallas kernels, per_device(): pl.pallas_call(functools.partial(force_terms, counts, depth, halves), out...  9.08 us
    pallas_call x1, Pallas kernels, per_device(): pl.pallas_call(functools.partial(expand, halves), out_shape=jax.ShapeDtyp...  0.86 us

profile of v5, /device:TPU:0, one launch (start us, length us, event | category | flops | bytes accessed | tf_op | source)
XLA Modules:
  0.0 9.9 jit_solution(2029151877097120613)
XLA Ops:
  0.0 9.1 %force_terms.1.acc = f32[512,128]{1,0:T(8,128)S(1)} custom-call(f32[4,2,3,3,16,128]{5,4,3,2,1,0:T(8,128)} %bitcast.2), custom_call_target="tpu_custom_call" | custom-call | tf_op jit(solution)/shard_map/force_terms/pallas_call | solution.py:806
  9.1 0.9 %expand.1 = f32[4,2,3,3,16,128]{5,4,3,2,1,0:T(8,128)} custom-call(f32[512,128]{1,0:T(8,128)S(1)} %force_terms.1.acc), custom_call_target="tpu_custom_call" | custom-call | tf_op jit(solution)/shard_map/expand/pallas_call | solution.py:826

commit v6 on v5

--- a/solution.py
+++ b/solution.py
@@ -128,14 +128,18 @@
     br, bi = (sr * xr - si * xi) * scale, (sr * xi + si * xr) * scale
     second_r = [pick(br, qr, pr), pick(pr, br, qr), pick(qr, pr, br)]
     second_i = [pick(bi, qi, pi), pick(pi, bi, qi), pick(qi, pi, bi)]
-    third_r, third_i = third_row([real, second_r], [imag, second_i])
-    return [[real, second_r, third_r], [imag, second_i, third_i]]
+    return [[real, second_r], [imag, second_i]]
+
+
+def with_third(rows):
+    third_r, third_i = third_row(*rows)
+    return [rows[0] + [third_r], rows[1] + [third_i]]
 
 
 def mail(depth, halves):
     up = lambda a, b: -(-a // b) * SUB
     per, yg = SUB // depth, LANES // NX
-    t, z, y = up(12, per), up(12, depth) * halves, up(36, yg) * halves
+    z, y = up(10 * halves, depth), up(36, yg) * halves
     short = up(10, per)
     groups = (
         ((("low", 2), y),),
@@ -143,11 +147,9 @@
         ((("low", 1, 0), z),),
         ((("low", 1, 2), z),),
         ((("high", 2), 3 * up(12 * halves, yg)),),
-        ((("high", 1, 3), z), (("high", 1, 0), z), (("high", 1, 2), z)),
-        ((("low", 0, 3), t),),
-        ((("low", 0, 1), t), (("low", 0, 2), t)),
+        ((("high", 1, 3), z), (("high", 1, 0), z), (("high", 1, 2), z), (("high", 0, 3), short)),
+        ((("low", 0, 3), short), (("low", 0, 1), short), (("low", 0, 2), short)),
         (((2, 1), SUB * halves), ((1, 2), SUB * halves), ((1, 0), 2 * SUB), ((2, 0), SUB)),
-        ((("high", 0, 3), short),),
         (((0, 1), 2 * SUB), ((0, 2), SUB)),
         ((("high", 0, "pair"), 10 * SUB),),
     )
@@ -287,21 +289,16 @@
         return total
 
     def pack_t(m):
-        cs = comps(m)
-        for c0 in range(0, 12, g.per):
-            put(
-                ("low", 0, m), c0 // g.per * SUB,
-                merge([g.rows(load(*cs[c0 + k], 0), depth * k) for k in range(g.per)], g.row, depth),
-            )
+        v = shortened([load(*c, 0) for c in comps(m)])
+        for c0 in range(0, 10, g.per):
+            ks = range(min(g.per, 10 - c0))
+            put(("low", 0, m), c0 // g.per * SUB, merge([g.rows(v[c0 + k], depth * k) for k in ks], g.row, depth))
 
     def pack_z(m):
-        cs = comps(m)
-        for c0 in range(0, 12, depth):
-            for h in range(halves):
-                put(
-                    ("low", 1, m), (c0 // depth * halves + h) * SUB,
-                    merge([g.rows(load(*cs[c0 + k], h), k) for k in range(depth)], g.zrow, 1),
-                )
+        v = [x for h in range(halves) for x in shortened([load(*c, h) for c in comps(m)])]
+        for c0 in range(0, len(v), depth):
+            ks = range(min(depth, len(v) - c0))
+            put(("low", 1, m), c0 // depth * SUB, merge([g.rows(v[c0 + k], k) for k in ks], g.zrow, 1))
 
     def pack_y():
         cs = all_comps(2)
@@ -326,12 +323,17 @@
         for c, (v, w) in enumerate(zip(shortened(one), shortened(two))):
             put(("high", 0, "pair"), c * SUB, jnp.where(g.row >= depth, g.rows(w, 2 * depth), g.rows(v, depth)))
 
-    def pack_vz(m, h, v):
-        for c0 in range(0, 12, depth):
+    def pack_vz(m, v):
+        for c0 in range(0, len(v), depth):
+            ks = range(min(depth, len(v) - c0))
             put(
-                ("high", 1, m), (c0 // depth * halves + h) * SUB,
-                merge([g.rows(v[c0 + k], k + 1 - depth) for k in range(depth)], g.zrow, 1),
+                ("high", 1, m), c0 // depth * SUB,
+                merge([g.rows(v[c0 + k], k + 1 - depth) for k in ks], g.zrow, 1),
             )
+
+    def got_z(side, m, h, c, row):
+        n = 10 * h + c
+        return g.rows(got((side, 1, m), n // depth * SUB), row - n % depth)
 
     def pack_vy(m, v):
         n = places["high", 2][1] // 3
@@ -524,8 +526,7 @@
                 prepare(nu, mu, h, 2)
         for d, m in ((mu, nu), (nu, mu)):
             if d == 1:
-                for h in range(halves):
-                    pack_vz(m, h, lifted[d, m, h])
+                pack_vz(m, [x for h in range(halves) for x in shortened(lifted[d, m, h])])
             elif d == 2:
                 pack_vy(m, [x for h in range(halves) for x in lifted[d, m, h]])
 
@@ -546,8 +547,8 @@
     lift(0, 1)
     lift(1, 2)
     pl.when(jnp.logical_not(at_end))(greeted)
-    for m in (3, 0, 2):
-        high[1, m].start()
+    above_z = [high[1, m] for m in (3, 0, 2)]
+    start(above_z)
     lift(2, 3)
     lift(0, 2)
     high_y.start()
@@ -560,15 +561,19 @@
         if complete(d, h):
             return saved(ahead_s, ahead_slot[m, d, h])
         index = {c: n for n, c in enumerate(all_comps(d))}
+        if d == 1:
+            edges = restored([got_z("low", m, h, c, depth - 1) for c in range(10)])
+        elif d == 0:
+            values = [got(("low", 0, m), c // g.per * SUB) for c in range(10)]
+            edges = restored(
+                [g.rows(v, SUB - depth - depth * (c % g.per)) for c, v in enumerate(values)]
+            )
 
         def get(part, i, j):
             v = ahead_s[ahead_slot[m, d, h], part, i, j]
             c = index[(m, part, i, j)]
-            k = c % 12
-            if d == 0:
-                edge = g.rows(got(("low", 0, m), k // g.per * SUB), SUB - depth - depth * (k % g.per))
-            elif d == 1:
-                edge = g.rows(got(("low", 1, m), (k // depth * halves + h) * SUB), depth - 1 - k % depth)
+            if d < 2:
+                edge = edges[part][i][j]
             else:
                 edge = g.lanes(
                     got(("low", 2), (c // g.ygroups * halves + h) * SUB), LANES - NX - NX * (c % g.ygroups)
@@ -626,8 +631,6 @@
     def lower(d, m, h):
         def get(part, i, j):
             c = part * 6 + i * 3 + j
-            if d == 1:
-                return g.rows(got(("high", 1, m), (c // depth * halves + h) * SUB), -(c % depth))
             n, k = places["high", 2][1] // 3, h * 12 + c
             r = others(2).index(m) * n + k // g.ygroups * SUB
             return g.lanes(got(("high", 2), r), -NX * (k % g.ygroups))
@@ -638,7 +641,9 @@
             left = matrix(m, h)
         if d == 0:
             values = [got(("high", 0, 3), c // g.per * SUB) for c in range(10)]
-            lifts = restored([g.rows(v, -depth * (c % g.per)) for c, v in enumerate(values)])
+            lifts = with_third(restored([g.rows(v, -depth * (c % g.per)) for c, v in enumerate(values)]))
+        elif d == 1:
+            lifts = with_third(restored([got_z("high", m, h, c, 0) for c in range(10)]))
         else:
             lifts = complete_rows(get)
         q = projected(left, lifts, right_h=True)
@@ -671,7 +676,7 @@
         )
 
     def pair_lower():
-        lifts = restored([got(("high", 0, "pair"), c * SUB) for c in range(10)])
+        lifts = with_third(restored([got(("high", 0, "pair"), c * SUB) for c in range(10)]))
         q = projected(saved(fixed_s, pair_slot), lifts, right_h=True)
         for c in range(8):
             add(1, c, 0, jnp.where(g.row < depth, q[c], 0.0))
@@ -710,6 +715,7 @@
     def t_part():
         arrived(("low", 0, 3))
         plane(0, 3, last)
+        plane(0, 1, last)
 
     def corner_part():
         answers(3)
@@ -718,18 +724,24 @@
 
     for h in range(last):
         plane(0, 3, h)
+    def cross_part():
+        arrived(("low", 1, 2))
+        for h in range(halves):
+            plane(1, 2, h)
+
+    near = me[0] == 0
+
     @pl.when(even)
     def _():
         y_part()
         around_part()
         z_part()
         rest_part()
+        pl.when(near)(t_part)
         corner_part()
-        t_part()
-        arrived(("low", 1, 2))
-        for h in range(halves):
-            plane(1, 2, h)
+        cross_part()
         high_y_part()
+        pl.when(jnp.logical_not(near))(t_part)
 
     @pl.when(jnp.logical_not(even))
     def _():
@@ -737,15 +749,12 @@
         around_part()
         rest_part()
         high_y_part()
+        pl.when(near)(t_part)
         corner_part()
-        t_part()
         y_part()
-        arrived(("low", 1, 2))
-        for h in range(halves):
-            plane(1, 2, h)
-
-    arrived(("low", 0, 1))
-    plane(0, 1, last)
+        cross_part()
+        pl.when(jnp.logical_not(near))(t_part)
+
     plane(0, 2, last)
     arrived((2, 1))
     for h in range(halves):
@@ -760,7 +769,6 @@
     for m in (3, 0, 2):
         for h in range(halves):
             lower(1, m, h)
-    arrived(("high", 0, 3))
     lower(0, 3, 0)
     arrived((0, 1))
     pair_fix()

time: 10.1 us -> 10 us (0.990)
  Pallas kernels: 9.94 us -> 9.8 us
    pallas_call x1, Pallas kernels: 9.08 us -> 8.95 us  [per_device(): pl.pallas_call(functools.partial(force_terms, counts, depth, halves), out...]
where the time goes in v6:
time: 10 us; the launch traced here: 9.81 us
  Pallas kernels  9.8 us (98%)
    pallas_call x1, Pallas kernels, per_device(): pl.pallas_call(functools.partial(force_terms, counts, depth, halves), out...  8.95 us
    pallas_call x1, Pallas kernels, per_device(): pl.pallas_call(functools.partial(expand, halves), out_shape=jax.ShapeDtyp...  0.86 us

profile of v6, /device:TPU:0, one launch (start us, length us, event | category | flops | bytes accessed | tf_op | source)
XLA Modules:
  0.0 9.8 jit_solution(12875878950034888500)
XLA Ops:
  0.0 8.9 %force_terms.1.acc = f32[512,128]{1,0:T(8,128)S(1)} custom-call(f32[4,2,3,3,16,128]{5,4,3,2,1,0:T(8,128)} %bitcast.2), custom_call_target="tpu_custom_call" | custom-call | tf_op jit(solution)/shard_map/force_terms/pallas_call | solution.py:814
  9.0 0.9 %expand.1 = f32[4,2,3,3,16,128]{5,4,3,2,1,0:T(8,128)} custom-call(f32[512,128]{1,0:T(8,128)S(1)} %force_terms.1.acc), custom_call_target="tpu_custom_call" | custom-call | tf_op jit(solution)/shard_map/expand/pallas_call | solution.py:834

commit v7 on v6

--- a/solution.py
+++ b/solution.py
@@ -175,17 +175,19 @@
     cut = last * SUB
     cut = last * SUB
 
-    def loads(m, p, from_last):
+    def loads(m, p, from_last, sem):
         rows = slice(cut, None) if from_last else slice(0, cut)
         return pltpu.make_async_copy(
-            hbm.at[m, p, :, :, rows], u.at[m, p, :, :, rows], load_sem.at[1 - from_last]
+            hbm.at[m, p, :, :, rows], u.at[m, p, :, :, rows], load_sem.at[sem]
         )
 
-    for from_last in (1, 0):
+    for from_last in (True, False):
         for m in (0, 3, 2, 1):
             for p in range(2):
-                loads(m, p, from_last).start()
-    load_last, load_rest = loads(slice(None), slice(None), 1), loads(slice(None), slice(None), 0)
+                loads(m, p, from_last, (1 if m else 0) if from_last else 2).start()
+    load_time = loads(0, slice(None), True, 0)
+    load_last = loads(slice(1, None), slice(None), True, 1)
+    load_rest = loads(slice(None), slice(None), False, 2)
 
     def peer(kind, sign):
         where = list(me)
@@ -493,10 +495,11 @@
         early(2, -1, [low_y])
 
     acc[...] = jnp.zeros_like(acc)
-    load_last.wait()
+    load_time.wait()
     for d in (1, 2):
         pack_corner(0, d)
         early(*CORNERS[0, d], [corners[0, d]])
+    load_last.wait()
     pl.when(jnp.logical_not(at_end))(faces)
     pack_vt(transported(local_product(0, 3, last), 0, 3, last, False))
     early(0, 1, [high[0, 3]])
@@ -675,8 +678,10 @@
             [[[jnp.where(edge, moved[p][i][j], own[p][i][j]) for j in range(3)] for i in range(3)] for p in range(2)],
         )
 
-    def pair_lower():
-        lifts = with_third(restored([got(("high", 0, "pair"), c * SUB) for c in range(10)]))
+    def pair_lift():
+        return with_third(restored([got(("high", 0, "pair"), c * SUB) for c in range(10)]))
+
+    def pair_lower(lifts):
         q = projected(saved(fixed_s, pair_slot), lifts, right_h=True)
         for c in range(8):
             add(1, c, 0, jnp.where(g.row < depth, q[c], 0.0))
@@ -770,10 +775,11 @@
         for h in range(halves):
             lower(1, m, h)
     lower(0, 3, 0)
+    arrived(("high", 0, "pair"))
+    lifts = pair_lift()
     arrived((0, 1))
     pair_fix()
-    arrived(("high", 0, "pair"))
-    pair_lower()
+    pair_lower(lifts)
     remote(0, spans[-1][1], 0, 0, 1).wait_send()
 
 
@@ -823,7 +829,7 @@
             vmem(3 + 2 * halves, 2, 3, 3, SUB),
             vmem(spans[-1][1]),
             vmem(spans[-1][1]),
-            pltpu.SemaphoreType.DMA((2,)),
+            pltpu.SemaphoreType.DMA((3,)),
             pltpu.SemaphoreType.DMA((1,)),
             pltpu.SemaphoreType.DMA((len(spans),)),
             pltpu.SemaphoreType.REGULAR((4,)),

time: 10 us -> 9.91 us (level)
  no operation moved by 1% of the time
where the time goes in v7:
time: 9.91 us; the launch traced here: 9.72 us
  Pallas kernels  9.71 us (98%)
    pallas_call x1, Pallas kernels, per_device(): pl.pallas_call(functools.partial(force_terms, counts, depth, halves), out...  8.85 us
    pallas_call x1, Pallas kernels, per_device(): pl.pallas_call(functools.partial(expand, halves), out_shape=jax.ShapeDtyp...  0.86 us

profile of v7, /device:TPU:0, one launch (start us, length us, event | category | flops | bytes accessed | tf_op | source)
XLA Modules:
  0.0 9.7 jit_solution(11392843637222935629)
XLA Ops:
  0.0 8.9 %force_terms.1.acc = f32[512,128]{1,0:T(8,128)S(1)} custom-call(f32[4,2,3,3,16,128]{5,4,3,2,1,0:T(8,128)} %bitcast.2), custom_call_target="tpu_custom_call" | custom-call | tf_op jit(solution)/shard_map/force_terms/pallas_call | solution.py:820
  8.9 0.9 %expand.1 = f32[4,2,3,3,16,128]{5,4,3,2,1,0:T(8,128)} custom-call(f32[512,128]{1,0:T(8,128)S(1)} %force_terms.1.acc), custom_call_target="tpu_custom_call" | custom-call | tf_op jit(solution)/shard_map/expand/pallas_call | solution.py:840

commit v8 on v7

--- a/solution.py
+++ b/solution.py
@@ -165,7 +165,7 @@
 
 def force_terms(
     counts, depth, halves, hbm, acc,
-    u, ahead_s, local_s, fixed_s, outbox, inbox, load_sem, send, recv, ready,
+    u, ahead_s, local_s, fixed_s, outbox, inbox, recv, ready, load_sem, send,
 ):
     g = Lattice(depth)
     last = halves - 1
@@ -817,8 +817,16 @@
     spans = mail(depth, halves)[1]
     vmem = lambda *s: pltpu.VMEM(s + (LANES,), jnp.float32)
     shape = links.shape[:4] + (sites, flat)
+
+    def kernel(*refs):
+        pl.run_scoped(
+            functools.partial(force_terms, counts, depth, halves, *refs),
+            pltpu.SemaphoreType.DMA((3,)),
+            pltpu.SemaphoreType.DMA((1,)),
+        )
+
     terms = pl.pallas_call(
-        functools.partial(force_terms, counts, depth, halves),
+        kernel,
         out_shape=pltpu.VMEM((32 * sites, flat), jnp.float32),
         in_specs=[pl.BlockSpec(memory_space=pl.ANY)],
         out_specs=pl.BlockSpec(memory_space=pltpu.VMEM),
@@ -829,8 +837,6 @@
             vmem(3 + 2 * halves, 2, 3, 3, SUB),
             vmem(spans[-1][1]),
             vmem(spans[-1][1]),
-            pltpu.SemaphoreType.DMA((3,)),
-            pltpu.SemaphoreType.DMA((1,)),
             pltpu.SemaphoreType.DMA((len(spans),)),
             pltpu.SemaphoreType.REGULAR((4,)),
         ],

time: 9.91 us -> 9.88 us (level)
  no operation moved by 1% of the time
where the time goes in v8:
time: 9.88 us; the launch traced here: 9.68 us
  Pallas kernels  9.67 us (98%)
    pallas_call x1, Pallas kernels, per_device(): pl.pallas_call(kernel, out_shape=pltpu.VMEM((32 * sites, flat), jnp.float...  8.82 us
    pallas_call x1, Pallas kernels, per_device(): pl.pallas_call(functools.partial(expand, halves), out_shape=jax.ShapeDtyp...  0.86 us

profile of v8, /device:TPU:0, one launch (start us, length us, event | category | flops | bytes accessed | tf_op | source)
XLA Modules:
  0.0 9.7 jit_solution(2105577235608008669)
XLA Ops:
  0.0 8.8 %force_terms.1.acc = f32[512,128]{1,0:T(8,128)S(1)} custom-call(f32[4,2,3,3,16,128]{5,4,3,2,1,0:T(8,128)} %bitcast.2), custom_call_target="tpu_custom_call" | custom-call | tf_op jit(solution)/shard_map/force_terms/pallas_call | solution.py:828
  8.8 0.9 %expand.1 = f32[4,2,3,3,16,128]{5,4,3,2,1,0:T(8,128)} custom-call(f32[512,128]{1,0:T(8,128)S(1)} %force_terms.1.acc), custom_call_target="tpu_custom_call" | custom-call | tf_op jit(solution)/shard_map/expand/pallas_call | solution.py:846
